TPU v7x, 32 devices: a whole 2x2x4 slice. The times are simulated.
32 devices in a mesh: section: 4 (over x, core), dp: 8 (over z, y).
Axes of the slice: x: 2, y: 2, z: 4, core: 2. Of those that a mesh axis runs over, the one named last changes fastest.
Arguments:
- clean_latent: float32 [64, 256], P('dp'), may hold values from -6 to 6
- noise_draw: float32 [64, 256], P('dp'), may hold values from -6 to 6
- step_index: int32 [64], P('dp'), may hold values from 250 to 1000
- labels: int32 [64], P('dp'), may hold values from 0 to 999
- guide_level: int32 [64], P('dp'), may hold values from 0 to 8
- class_table: bfloat16 [1001, 1152], replicated, may hold values from -6 to 6
- embed_in: bfloat16 [16, 1152], replicated, may hold values from -1.5 to 1.5
- embed_out: bfloat16 [1152, 16], replicated, may hold values from -0.1875 to 0.1875
- teacher_up: bfloat16 [4, 1152, 2304], P('section', 'dp'), may hold values from -0.1875 to 0.1875
- teacher_down: bfloat16 [4, 2304, 1152], P('section', 'dp'), may hold values from -0.125 to 0.125
- teacher_gain: float32 [4, 3, 1152], P('section'), may hold values from -3 to 3
- teacher_bias: float32 [4, 3, 1152], P('section'), may hold values from -3 to 3
- student_up: bfloat16 [1152, 4608], P(None, 'section'), may hold values from -0.1875 to 0.1875
- student_down: bfloat16 [4608, 1152], P('section'), may hold values from -0.09375 to 0.09375
- student_gain: float32 [3, 1152], replicated, may hold values from -3 to 3
- student_bias: float32 [3, 1152], replicated, may hold values from -3 to 3
- guide_vec: float32 [1152], replicated, may hold values from -3 to 3
Outputs:
- distill_target: float32 [64, 256], P('dp')
- grad_up: float32 [1152, 4608], P('dp', 'section')
- grad_down: float32 [4608, 1152], P(('section', 'dp'))
All inputs are finite; a program needn't handle non-finite values.
Results may differ from a plain program's by a relative error of at most 0.017.
Values may be sent and summed in bfloat16 or wider, within the bound.
A program may use at most 128 MiB of HBM per device.

v0:
```python
import functools
import math

import jax
import jax.numpy as jnp
from jax import lax
from jax.experimental import pallas as pl
from jax.experimental.pallas import tpu as pltpu
from jax.sharding import PartitionSpec as P

CH = 16
TSTEPS = 1000
STRIDE = 125


norm_eps = 1e-06


def shifted(shard, axis, by):
    length = lax.axis_size(axis)
    return lax.ppermute(shard, axis, [(i, (i + by) % length) for i in range(length)])


def from_root(shard, axis, root):
    mine = lax.axis_index(axis) == root
    return lax.psum(jnp.where(mine, shard, jnp.zeros_like(shard)), axis)


def layer_norm(values):
    center = values - jnp.mean(values, axis=-1, keepdims=True)
    spread = jnp.mean(center * center, axis=-1, keepdims=True)
    return center * lax.rsqrt(spread + norm_eps)


def sinusoid(step_ids, model_width):
    half_width = model_width // 2
    frequency = jnp.exp(-math.log(10000.0) * jnp.arange(half_width, dtype=jnp.float32) / half_width)
    phase_arg = step_ids.astype(jnp.float32)[:, None] * frequency[None, :]
    return jnp.concatenate([jnp.cos(phase_arg), jnp.sin(phase_arg)], axis=-1)


def plan(step_ids):
    angle_t = 0.5 * math.pi / TSTEPS * step_ids.astype(jnp.float32)
    return (jnp.cos(angle_t), jnp.sin(angle_t))


def embed_tokens(latent, embed_in):
    leading = latent.shape[0]
    patches = latent.reshape(leading * (latent.shape[1] // CH), CH).astype(jnp.bfloat16)
    tokens = jnp.dot(patches, embed_in, preferred_element_type=jnp.float32)
    return tokens.reshape(leading, latent.shape[1] // CH, embed_in.shape[1]).astype(jnp.bfloat16)


def mlp_block(inputs, modulation, up_proj, down_proj):
    groups, seq_len, model_width = inputs.shape
    residual_in = inputs.astype(jnp.float32)
    shift_rows = modulation[:, 0, None, :]
    scale_rows = modulation[:, 1, None, :]
    gate_rows = modulation[:, 2, None, :]
    normed = (layer_norm(residual_in) * (1.0 + scale_rows) + shift_rows).astype(jnp.bfloat16)
    pre_act = jnp.dot(
        normed.reshape(groups * seq_len, model_width), up_proj, preferred_element_type=jnp.float32
    )
    hidden = jax.nn.gelu(pre_act, approximate=True).astype(jnp.bfloat16)
    mixed = jnp.dot(hidden, down_proj, preferred_element_type=jnp.float32).reshape(
        groups, seq_len, model_width
    )
    return (residual_in + gate_rows * mixed).astype(jnp.bfloat16)


def velocity(states, embed_out):
    groups, seq_len, model_width = states.shape
    normed = layer_norm(states.astype(jnp.float32)).astype(jnp.bfloat16)
    result = jnp.dot(
        normed.reshape(groups * seq_len, model_width), embed_out, preferred_element_type=jnp.float32
    )
    return result.reshape(groups, seq_len * embed_out.shape[1])


def ddim_step(latent, predicted, time_now, time_next):
    alpha_now, sigma_now = plan(time_now)
    alpha_next, sigma_next = plan(time_next)
    clean_est = alpha_now[:, None] * latent - sigma_now[:, None] * predicted
    noise_est = sigma_now[:, None] * latent + alpha_now[:, None] * predicted
    return alpha_next[:, None] * clean_est + sigma_next[:, None] * noise_est


def gelu_slope(pre_act):
    return jax.vjp(lambda inner: jax.nn.gelu(inner, approximate=True), pre_act)[1](
        jnp.ones_like(pre_act)
    )[0]


def run_chunks(count, one, operands, shared):
    if count == 1:
        return one(operands, *shared)

    def step(carry, piece):
        out = one(piece, *shared)
        return (carry[0] + out[0], carry[1] + out[1]), None

    split = [a.reshape((count, a.shape[0] // count) + a.shape[1:]) for a in operands]
    shapes = jax.eval_shape(one, [a[0] for a in split], *shared)
    zeros = tuple(jnp.zeros(s.shape, s.dtype) for s in shapes)
    return lax.scan(step, zeros, split)[0]


def teacher_chain(first_in, noised, guidance, step_index, mods, up, down, embed_in, embed_out):
    section_count = lax.axis_size("section")
    section_at = lax.axis_index("section")
    micro, seq_len, model_width = first_in.shape

    def paired(tokens):
        return jnp.broadcast_to(tokens[:, None], (micro, 2, seq_len, model_width)).reshape(
            2 * micro, seq_len, model_width
        )

    latent = noised
    states = paired(first_in)
    for which_step in range(2):
        mod = mods[which_step].reshape(2 * micro, 3, model_width)
        if which_step:
            states = paired(embed_tokens(latent, embed_in))
        for layer in range(section_count):
            states = mlp_block(states, mod, up, down)
            if layer < section_count - 1:
                states = lax.ppermute(states, "section", [(layer, layer + 1)])
        predicted = velocity(states, embed_out).reshape(micro, 2, -1)
        weight = guidance[:, None]
        guided = (1.0 + weight) * predicted[:, 0] - weight * predicted[:, 1]
        time_now = step_index - which_step * STRIDE
        stepped = ddim_step(latent, guided, time_now, time_now - STRIDE)
        if which_step == 0:
            returned = lax.ppermute(
                stepped, "section", [(section_count - 1, 0)]
            )
            latent = jnp.where(section_at == section_count - 1, stepped, returned)
    return stepped


def chunked_mlp(normed, up_ref, down_ref, width):
    def piece(j, total):
        at = pl.ds(pl.multiple_of(j * width, width), width)
        hidden = jax.nn.gelu(
            jnp.dot(normed, up_ref[:, at], preferred_element_type=jnp.float32), approximate=True
        ).astype(jnp.bfloat16)
        return total + jnp.dot(hidden, down_ref[at, :], preferred_element_type=jnp.float32)

    zero = jnp.zeros((normed.shape[0], down_ref.shape[1]), jnp.float32)
    return lax.fori_loop(0, up_ref.shape[1] // width, piece, zero, unroll=True)


def teacher_kernel(
    dims,
    up_shard, down_shard, packed_in, normed_own, stud_up, stud_down,
    mods, first_in, latent_in, coef, embed_in, embed_out,
    packed_all, mixed_all, target_all,
    up, down, parts, states, outs, velo, z_sem_buf, z_in,
    send, recv,
):
    section_count, dp_count, micro, seq_len = dims
    sec = lax.axis_index("section")
    me = lax.axis_index("dp")
    planes = dp_count // 2
    z, y = me // 2, me % 2
    z_up = lax.rem(z + 1, planes)
    z_dn = lax.rem(z + planes - 1, planes)
    z_op = lax.rem(z + 2, planes)
    tail = section_count - 1

    def at(zz, yy):
        return zz * 2 + yy

    peer, above, below = at(z, 1 - y), at(z_up, y), at(z_dn, y)
    barrier = pltpu.get_barrier_semaphore()
    for k in range(1, dp_count):
        pl.semaphore_signal(
            barrier, inc=1, device_id={"dp": lax.rem(me + k, dp_count)},
            device_id_type=pl.DeviceIdType.MESH,
        )
    for k in range(1, section_count):
        pl.semaphore_signal(
            barrier, inc=1, device_id={"section": lax.rem(sec + k, section_count)},
            device_id_type=pl.DeviceIdType.MESH,
        )
    pl.semaphore_wait(barrier, dp_count + section_count - 2)

    count = [0]

    def copy(src, dst, **device):
        i = count[0]
        count[0] += 1
        return pltpu.make_async_remote_copy(
            src_ref=src, dst_ref=dst, send_sem=send.at[i], recv_sem=recv.at[i],
            device_id=device, device_id_type=pl.DeviceIdType.MESH,
        )

    ur, dr = up_shard.shape[0], down_shard.shape[0]
    ua = (ur // 32) * 16 + 16 * ((ur // 16) % 2)
    da = (dr // 32) * 16

    def rows(ref, size, who, lo=0, n=None):
        n = size if n is None else n
        return ref.at[pl.ds(pl.multiple_of(who * size + lo, 16), n)]

    u, w = functools.partial(rows, up, ur), functools.partial(rows, down, dr)

    def go(c):
        c.start()
        return c

    sent = []

    def ship(src, dst, **device):
        c = go(copy(src, dst, **device))
        sent.append(c)
        return c

    own_slot_rows = micro * seq_len
    packs = []
    for k in range(1, dp_count):
        packs.append(
            ship(packed_in, packed_all.at[me], dp=lax.rem(me + k, dp_count))
        )
    u_up = ship(up_shard, u(me), dp=above)
    u_dn = ship(up_shard, u(me), dp=below)
    w_y = ship(down_shard, w(me), dp=peer)
    w_up = ship(down_shard, w(me), dp=above)
    w_dn = ship(down_shard, w(me), dp=below)
    u_y = ship(up_shard, u(me), dp=peer)
    packed_all[me] = packed_in[...]
    up[pl.ds(pl.multiple_of(me * ur, 16), ur)] = up_shard[...]
    down[pl.ds(pl.multiple_of(me * dr, 16), dr)] = down_shard[...]

    parts[sec] = chunked_mlp(normed_own[...], stud_up, stud_down, 384).astype(jnp.bfloat16)
    part_copies = [
        ship(parts.at[sec], parts.at[sec], section=lax.rem(sec + k, section_count))
        for k in range(1, section_count)
    ]

    u_up.wait_recv()
    f_uu = ship(u(below, 0, ua), u(below, 0, ua), dp=above)
    f_uy1 = ship(u(below), u(below), dp=peer)
    u_dn.wait_recv()
    f_ud = ship(u(above, ua, ur - ua), u(above, ua, ur - ua), dp=below)
    f_uy2 = ship(u(above), u(above), dp=peer)
    w_y.wait_recv()
    v_up = ship(w(peer), w(peer), dp=above)
    v_dn = ship(w(peer), w(peer), dp=below)
    w_up.wait_recv()
    f_wu = ship(w(below, 0, da), w(below, 0, da), dp=above)
    w_dn.wait_recv()
    f_wd = ship(w(above, da, dr - da), w(above, da, dr - da), dp=below)
    f_uu.wait_recv()
    f_ud.wait_recv()
    opp = at(z_op, y)
    f_uy3 = ship(u(opp), u(opp), dp=peer)
    v_up.wait_recv()
    pb = at(z_dn, 1 - y)
    g_wu = ship(w(pb, 0, da), w(pb, 0, da), dp=above)
    v_dn.wait_recv()
    pa = at(z_up, 1 - y)
    g_wd = ship(w(pa, da, dr - da), w(pa, da, dr - da), dp=below)

    for c in part_copies:
        c.wait_recv()
    total = parts[0].astype(jnp.float32)
    for k in range(1, section_count):
        total = total + parts[k].astype(jnp.float32)
    mixed_all[me] = total.astype(jnp.bfloat16)
    for c in (u_y, f_wu, f_wd, f_uy1, f_uy2, f_uy3, g_wu, g_wd):
        c.wait_recv()
    mix_copies = [
        ship(mixed_all.at[me], mixed_all.at[me], dp=lax.rem(me + k, dp_count))
        for k in range(1, dp_count)
    ]

    width = first_in.shape[1]
    nxt = lax.rem(sec + 1, section_count)
    moves = [copy(outs.at[i], states.at[i], section=nxt) for i in range(4)]
    z_move = copy(z_sem_buf, z_in, section=0)
    goal_copies = [
        copy(target_all.at[me], target_all.at[me], dp=lax.rem(me + k, dp_count))
        for k in range(1, dp_count)
    ]
    final_copies = [
        copy(target_all, target_all, section=k) for k in range(tail)
    ]

    for step in range(2):
        if step == 1:
            @pl.when(sec == 0)
            def _():
                z_move.wait_recv()

        for half in range(2):
            slot = 2 * step + half

            @pl.when(sec == 0)
            def _():
                if step == 0:
                    states[slot] = first_in[...]
                else:
                    states[slot] = lax.dot_general(
                        z_in[...].astype(jnp.bfloat16), embed_in[...], (((0,), (0,)), ((), ())),
                        preferred_element_type=jnp.float32,
                    ).astype(jnp.bfloat16)

            @pl.when(sec > 0)
            def _():
                moves[slot].wait_recv()

            residual = states[slot].astype(jnp.float32)
            shift = mods[step, half, 0][:, None, :]
            scale = mods[step, half, 1][:, None, :]
            gate = mods[step, half, 2][:, None, :]
            cube = layer_norm(residual).reshape(micro, seq_len, width)
            normed = (cube * (1.0 + scale) + shift).astype(jnp.bfloat16)
            mixed = chunked_mlp(normed.reshape(micro * seq_len, width), up, down, 768)
            out = residual.reshape(micro, seq_len, width) + gate * mixed.reshape(
                micro, seq_len, width
            )
            outs[slot] = out.reshape(micro * seq_len, width).astype(jnp.bfloat16)

            @pl.when(sec < tail)
            def _():
                moves[slot].start()

            @pl.when(sec == tail)
            def _():
                last = layer_norm(outs[slot].astype(jnp.float32)).astype(jnp.bfloat16)
                velo[half] = lax.dot_general(
                    embed_out[...], last, (((0,), (1,)), ((), ())),
                    preferred_element_type=jnp.float32,
                )

        @pl.when(sec == tail)
        def _():
            level = coef[4:5, :]
            guided = (1.0 + level) * velo[0] - level * velo[1]
            before = latent_in[...] if step == 0 else z_sem_buf[...]
            after = coef[2 * step : 2 * step + 1, :] * before + coef[
                2 * step + 1 : 2 * step + 2, :
            ] * guided
            if step == 0:
                z_sem_buf[...] = after
                z_move.start()
                z_move.wait_send()
            else:
                target_all[me] = coef[5:6, :] * after + coef[6:7, :] * latent_in[...]

    @pl.when(sec == tail)
    def _():
        for c in goal_copies:
            c.start()
        for c in goal_copies:
            c.wait()
        for c in final_copies:
            c.start()
        for c in final_copies:
            c.wait_send()

    for k in range(tail):
        @pl.when(sec == k)
        def _():
            final_copies[k].wait_recv()

    @pl.when(sec < tail)
    def _():
        for c in moves:
            c.wait_send()

    for c in packs + mix_copies:
        c.wait_recv()
    for c in sent:
        c.wait_send()


def teacher_call(dims, operands):
    section_count, dp_count, micro, seq_len = dims
    up_shard, down_shard = operands[0], operands[1]
    width = up_shard.shape[1]
    model_width = down_shard.shape[1]
    row_count = micro * seq_len
    copies = 3 * (dp_count - 1) + 2 * section_count + 64
    block = (row_count, model_width)
    vmem = pl.BlockSpec(memory_space=pltpu.VMEM)
    return pl.pallas_call(
        functools.partial(teacher_kernel, dims),
        out_shape=(
            jax.ShapeDtypeStruct((dp_count,) + operands[2].shape, jnp.float32),
            jax.ShapeDtypeStruct((dp_count,) + block, jnp.bfloat16),
            jax.ShapeDtypeStruct((dp_count, CH, row_count), jnp.float32),
        ),
        in_specs=[vmem] * len(operands),
        out_specs=(vmem,) * 3,
        scratch_shapes=[
            pltpu.VMEM((up_shard.shape[0] * dp_count, width), jnp.bfloat16),
            pltpu.VMEM((down_shard.shape[0] * dp_count, model_width), jnp.bfloat16),
            pltpu.VMEM((section_count,) + block, jnp.bfloat16),
            pltpu.VMEM((4,) + block, jnp.bfloat16),
            pltpu.VMEM((4,) + block, jnp.bfloat16),
            pltpu.VMEM((2, CH, row_count), jnp.float32),
            pltpu.VMEM((CH, row_count), jnp.float32),
            pltpu.VMEM((CH, row_count), jnp.float32),
            pltpu.SemaphoreType.DMA((copies,)),
            pltpu.SemaphoreType.DMA((copies,)),
        ],
        compiler_params=pltpu.CompilerParams(
            collective_id=0, has_side_effects=True, vmem_limit_bytes=56 << 20
        ),
    )(*operands)


def body(
    clean_latent,
    noise_draw,
    step_index,
    labels,
    guide_level,
    class_table,
    embed_in,
    embed_out,
    teacher_up,
    teacher_down,
    teacher_gain,
    teacher_bias,
    student_up,
    student_down,
    student_gain,
    student_bias,
    guide_vec,
):
    section_count = lax.axis_size("section")
    dp_count = lax.axis_size("dp")
    section_at = lax.axis_index("section")
    dp_at = lax.axis_index("dp")
    micro = clean_latent.shape[0]
    width = clean_latent.shape[1]
    seq_len = width // CH
    model_width = class_table.shape[1]
    fused = (
        dp_count == 8
        and section_count == 4
        and teacher_up.shape[1] % 16 == 0
        and teacher_down.shape[1] % 32 == 0
    )
    alpha_t, sigma_t = plan(step_index)
    noised = alpha_t[:, None] * clean_latent + sigma_t[:, None] * noise_draw
    guidance = 0.5 * guide_level.astype(jnp.float32)
    label_rows = jnp.take(class_table, labels, axis=0).astype(jnp.float32)
    null_row = class_table[class_table.shape[0] - 1].astype(jnp.float32)
    wave_rows = jnp.stack(
        [sinusoid(step_index - step_k * STRIDE, model_width) for step_k in range(2)]
    )
    conditions = jnp.stack(
        [wave_rows + label_rows[None], wave_rows + null_row[None, None, :]], axis=2
    )
    mods = (
        conditions[:, :, :, None, :] * teacher_gain[0][None, None, None]
        + teacher_bias[0][None, None, None]
    )
    first_in = embed_tokens(noised, embed_in)
    alpha_end, sigma_end = plan(step_index - 2 * STRIDE)
    sigma_ratio = sigma_end / sigma_t
    packed = jnp.concatenate(
        [
            noised,
            step_index.astype(jnp.float32)[:, None],
            labels.astype(jnp.float32)[:, None],
            guide_level.astype(jnp.float32)[:, None],
        ],
        axis=1,
    )
    def student_normed(noised, steps, labels, guidance):
        rows = noised.shape[0] * seq_len
        label_rows = jnp.take(class_table, labels, axis=0).astype(jnp.float32)
        cond = sinusoid(steps, model_width) + label_rows + guidance[:, None] * guide_vec[None, :]
        modulation = cond[:, None, :] * student_gain[None] + student_bias[None]
        residual_in = embed_tokens(noised, embed_in).astype(jnp.float32)
        normed = (
            (layer_norm(residual_in) * (1.0 + modulation[:, 1, None, :]) + modulation[:, 0, None, :])
            .astype(jnp.bfloat16)
            .reshape(rows, model_width)
        )
        return residual_in, modulation[:, 2, None, :], normed

    def student_front(noised, steps, labels, guidance, student_up):
        residual_in, gate_rows, normed = student_normed(noised, steps, labels, guidance)
        pre_act = jnp.dot(normed, student_up, preferred_element_type=jnp.float32)
        hidden = jax.nn.gelu(pre_act, approximate=True).astype(jnp.bfloat16)
        return residual_in, gate_rows, normed, pre_act, hidden

    total = micro * dp_count
    element_count = total * width
    up_share = model_width // dp_count
    down_share = student_down.shape[0] // dp_count

    goal_scale = 1.0 / (alpha_end - sigma_ratio * alpha_t)
    if fused:
        own_normed = student_normed(noised, step_index, labels, guidance)[2]
        pack_pad = -packed.shape[1] % 128
        packed = jnp.pad(packed, ((0, 0), (0, pack_pad)))
        coefs = []
        for step_k in range(2):
            alpha_k, sigma_k = plan(step_index - step_k * STRIDE)
            alpha_n, sigma_n = plan(step_index - (step_k + 1) * STRIDE)
            coefs += [alpha_n * alpha_k + sigma_n * sigma_k, sigma_n * alpha_k - alpha_n * sigma_k]
        coefs += [guidance, goal_scale, -sigma_ratio * goal_scale, guidance]
        coefs = jnp.repeat(jnp.stack(coefs), seq_len, axis=1)
        packed, all_mixed, all_target = teacher_call(
            (section_count, dp_count, micro, seq_len),
            (
                teacher_up[0],
                teacher_down[0],
                packed,
                own_normed,
                student_up,
                student_down,
                mods.transpose(0, 2, 3, 1, 4),
                first_in.reshape(micro * seq_len, model_width),
                noised.reshape(micro * seq_len, CH).T,
                coefs,
                embed_in,
                embed_out,
            ),
        )
        packed = packed.reshape(total, packed.shape[-1])
        all_target = all_target.transpose(0, 2, 1).reshape(total, width)
    else:
        up = lax.all_gather(teacher_up[0], "dp", axis=0, tiled=True)
        down = lax.all_gather(teacher_down[0], "dp", axis=0, tiled=True)
        ending = teacher_chain(
            first_in, noised, guidance, step_index, mods, up, down, embed_in, embed_out
        )
        goal_latent = (ending - sigma_ratio[:, None] * noised) * goal_scale[:, None]
        packed = lax.all_gather(packed, "dp", axis=0, tiled=True)
        own = student_front(noised, step_index, labels, guidance, student_up)
        partial_value = jnp.dot(own[4], student_down, preferred_element_type=jnp.float32)
        mixed = lax.psum(partial_value.astype(jnp.bfloat16), "section")
        all_mixed = lax.all_gather(mixed, "dp", axis=0, tiled=True)
        gathered = lax.all_gather(goal_latent, ("section", "dp"), axis=0, tiled=True)
        all_target = gathered[total * (section_count - 1):]
    all_mixed = all_mixed.reshape(total, seq_len, model_width)
    all_noised = packed[:, :width]
    all_steps = packed[:, width].astype(jnp.int32)
    all_labels = packed[:, width + 1].astype(jnp.int32)
    all_guidance = 0.5 * packed[:, width + 2]
    distill_target = lax.dynamic_slice_in_dim(all_target, dp_at * micro, micro, 0)

    def student_grads(operands, student_up, student_down):
        noised, steps, labels, guidance, mixed, target = operands
        count = noised.shape[0]
        rows = count * seq_len
        residual_in, gate_rows, normed, pre_act, hidden = student_front(
            noised, steps, labels, guidance, student_up
        )
        state_rows = residual_in + gate_rows * mixed.astype(jnp.float32)
        alpha_t, sigma_t = plan(steps)
        normed_out, pullback = jax.vjp(layer_norm, state_rows)
        predicted = jnp.dot(
            normed_out.astype(jnp.bfloat16).reshape(rows, model_width),
            embed_out,
            preferred_element_type=jnp.float32,
        ).reshape(count, width)
        estimate = alpha_t[:, None] * noised - sigma_t[:, None] * predicted
        weight = jnp.maximum(alpha_t * alpha_t / (sigma_t * sigma_t), 1.0)
        slope_pred = -2.0 / element_count * (sigma_t * weight)[:, None] * (estimate - target)
        back_norm = jnp.dot(
            slope_pred.reshape(rows, CH),
            embed_out.astype(jnp.float32).T,
            precision=lax.Precision.HIGHEST,
        )
        back_state = pullback(back_norm.reshape(count, seq_len, model_width))[0]
        back_part = (gate_rows * back_state).astype(jnp.bfloat16).reshape(rows, model_width)
        back_hidden = lax.dot_general(
            back_part, student_down, (((1,), (1,)), ((), ())), preferred_element_type=jnp.float32
        )
        back_pre = (back_hidden * gelu_slope(pre_act)).astype(jnp.bfloat16)
        normed_share = lax.dynamic_slice_in_dim(normed, dp_at * up_share, up_share, 1)
        hidden_share = lax.dynamic_slice_in_dim(hidden, dp_at * down_share, down_share, 1)
        contract_rows = (((0,), (0,)), ((), ()))
        return (
            lax.dot_general(
                normed_share, back_pre, contract_rows, preferred_element_type=jnp.float32
            ),
            lax.dot_general(
                hidden_share, back_part, contract_rows, preferred_element_type=jnp.float32
            ),
        )

    operands = [all_noised, all_steps, all_labels, all_guidance, all_mixed, all_target]
    grad_up, grad_down = run_chunks(
        max(1, dp_count // 8), student_grads, operands, (student_up, student_down)
    )
    return (distill_target, grad_up, grad_down)


def solution(mesh):
    return jax.shard_map(
        body,
        mesh=mesh,
        in_specs=(
            P("dp", None),
            P("dp", None),
            P("dp"),
            P("dp"),
            P("dp"),
            P(),
            P(),
            P(),
            P("section", "dp", None),
            P("section", "dp", None),
            P("section", None, None),
            P("section", None, None),
            P(None, "section"),
            P("section", None),
            P(),
            P(),
            P(),
        ),
        out_specs=(P("dp", None), P("dp", "section"), P(("section", "dp"), None)),
        check_vma=False,
    )
```

profile of v0, /device:TPU:0, one launch (start us, length us, event | category | flops | bytes accessed | tf_op | source)
XLA Modules:
  0.0 267.7 jit_solution(5675906421105171523)
XLA Ops:
  0.6 0.7 compare_and_fusion
  1.3 0.7 convert_bitcast_fusion
  2.0 0.7 compare_select_fusion.1
  2.7 0.7 add_convert_fusion
  3.4 0.1 copy.26
  3.5 0.1 copy.24
  3.6 0.1 copy.25
  3.7 0.8 multiply_bitcast_fusion
  4.5 0.7 convert_reduce_fusion.2
  5.3 0.8 fusion.59
  6.0 0.7 select_maximum_fusion.packed_in
  6.7 2.5 gather_fusion.1
  9.3 0.1 convert_element_type.123
  9.4 0.1 broadcast_in_dim.36
  9.4 0.7 reshape.275.coef
  10.1 0.1 select_convert_fusion
  10.2 0.7 copy_bitcast_fusion
  10.9 0.1 reshape.274
  11.0 0.7 copy.27
  11.7 0.2 multiply_cosine_fusion.1
  11.9 0.1 maximum_bitcast_fusion.1
  12.0 0.8 fusion.43
  12.8 0.8 multiply_add_fusion.2
  13.6 0.8 multiply_add_fusion.1.mods
  14.4 1.0 convert_reduce_fusion.1
  15.5 0.2 fusion.19
  15.7 0.0 copy-start.7
  15.7 1.0 fusion.22
  16.7 1.7 copy.28.embed_out
  18.4 197.8 %shard_map.184 = (f32[8,8,384]{2,1,0:T(8,128)}, bf16[8,128,1152]{2,1,0:T(8,128)(2,1)}, f32[8,16,128]{2,1,0:T(8,128)}) custom-call(bf16[144,2304]{1,0:T(8,128)(2,1)} %bitcast.90, bf16[288,1152]{1,0:T(8,128)(2,1)} %bitcast.91, f32[8,384]{1,0:T(8,128)} %select_maximum_fusion.packed_in, bf16[128,1152]{1,0:T(8,128)(2,1)} %bitcast.89, bf16[1152,1152]{1,0:T(8,128)(2,1)} %stud_up.1, ...), custom_call_target="tpu_custom_call" | custom-call | tf_op jit(solution)/shard_map/pallas_call | solution.py:388
  216.2 0.0 copy-start.8
  216.2 1.0 and_reduce_fusion
  217.1 0.9 fusion.46
  218.1 1.2 multiply_reduce_fusion.2
  219.3 0.8 slice.94
  220.1 0.1 copy.30
  220.3 0.0 copy-done.7
  220.3 0.7 gather_fusion
  221.0 0.3 copy.31
  221.3 0.6 multiply_cosine_fusion
  221.9 0.1 fusion.28
  222.1 1.0 copy.29
  223.1 0.2 reshape.276
  223.3 0.0 copy-start.10
  223.4 0.6 constant_dynamic-slice_fusion
  224.0 0.1 multiply_add_fusion
  224.0 0.8 slice_bitcast_fusion
  224.8 2.8 %fusion.13 = (f32[64,16]{1,0:T(8,128)S(1)}, bf16[64,16,1152]{2,1,0:T(8,128)(2,1)S(1)}) fusion(bf16[64,16,1152]{2,1,0:T(8,128)(2,1)} %bitcast.77, f32[64,1152]{1,0:T(8,128)S(1)} %get-tuple-element.25, bf16[64,16,16]{2,1,0:T(8,128)(2,1)S(1)} %copy.31, bf16[16,1152]{1,0:T(8,128)(2,1)S(1)} %copy-done.8), kind=kOutput, calls=%fused_computation.28 | convolution fusion | flops 44825600 | bytes 5087232 | tf_op jit(solution)/shard_map/dot_general | solution.py:50
  227.6 2.8 %multiply_reduce_fusion.1 = f32[64,16]{1,0:T(8,128)S(1)} fusion(f32[64,16]{1,0:T(8,128)S(1)} %broadcast_multiply_fusion, bf16[64,16,1152]{2,1,0:T(8,128)(2,1)} %bitcast.78, f32[64,1152]{1,0:T(8,128)S(1)} %get-tuple-element.25, bf16[64,16,1152]{2,1,0:T(8,128)(2,1)S(1)} %get-tuple-element.58), kind=kLoop, calls=%fused_computation.25 | loop fusion | flops 8256512 | bytes 5021696 | tf_op jit(solution)/shard_map/jvp()/reduce_sum | solution.py:31
  230.5 0.0 copy-done
  230.5 1.2 multiply_convert_fusion.1
  231.7 0.7 fusion.60
  232.4 0.9 reshape.280
  233.3 1.0 subtract_multiply_fusion
  234.3 0.8 copy.33
  235.1 1.2 copy.34
  236.3 4.9 %multiply_reduce_fusion = (f32[64,16]{1,0:T(8,128)S(1)}, f32[64,16]{1,0:T(8,128)S(1)}, f32[64,16,1152]{2,1,0:T(8,128)S(1)}) fusion(f32[64,16]{1,0:T(8,128)S(1)} %broadcast_multiply_fusion, bf16[64,16,1152]{2,1,0:T(8,128)(2,1)} %bitcast.79, f32[64,1152]{1,0:T(8,128)S(1)} %get-tuple-element.25, bf16[64,16,1152]{2,1,0:T(8,128)(2,1)S(1)} %get-tuple-element.58, ...), kind=kOutput, calls=%fused_computation.23 | convolution fusion | flops 235927552 | bytes 9846784 | tf_op jit(solution)/shard_map/dot_general | solution.py:569
  241.2 0.0 copy-start.6
  241.2 2.8 %fusion.26 = (f32[64,16]{1,0:T(8,128)S(1)}, f32[64,16]{1,0:T(8,128)S(1)}) fusion(f32[64,16]{1,0:T(8,128)S(1)} %multiply_multiply_fusion.2, f32[64,16]{1,0:T(8,128)S(1)} %broadcast_multiply_fusion, bf16[64,16,1152]{2,1,0:T(8,128)(2,1)S(1)} %bitcast.81, f32[64,1152]{1,0:T(8,128)S(1)} %get-tuple-element.25, bf16[64,16,1152]{2,1,0:T(8,128)(2,1)S(1)} %get-tuple-element.58, ...), kind=kLoop, calls=%fused_computation.47 | loop fusion | flops 15333376 | bytes 9756672 | tf_op jit(solution)/shard_map/transpose(jvp())/reduce_sum | solution.py:30
  244.0 0.0 copy-start.4
  244.1 4.2 %multiply_convert_fusion = (bf16[64,16,1152]{2,1,0:T(8,128)(2,1)}, bf16[64,16,1152]{2,1,0:T(8,128)(2,1)S(1)}) fusion(f32[64,16]{1,0:T(8,128)S(1)} %negate_multiply_fusion, f32[64,1152]{1,0:T(8,128)S(1)} %get-tuple-element.25, f32[64,16]{1,0:T(8,128)S(1)} %multiply_multiply_fusion.2, f32[64,16]{1,0:T(8,128)S(1)} %broadcast_multiply_fusion, ...), kind=kLoop, calls=%fused_computation.22 | loop fusion | flops 20054016 | bytes 15065088 | tf_op jit(solution)/shard_map/convert_element_type | solution.py:575
  248.3 6.0 %add_multiply_fusion = (f32[1024,1152]{1,0:T(8,128)}, f32[1024,1152]{1,0:T(8,128)}) fusion(bf16[1024,1152]{1,0:T(8,128)(2,1)S(1)} %bitcast.87, bf16[1152,1152]{1,0:T(8,128)(2,1)S(1)} %copy-done.4), kind=kOutput, calls=%fused_computation.26 | convolution fusion | flops 2726166528 | bytes 14450688 | tf_op jit(solution)/shard_map/dot_general | solution.py:490
  254.3 9.5 %fusion.15 = f32[144,1152]{1,0:T(8,128)} fusion(f32[1024,1152]{1,0:T(8,128)} %get-tuple-element.61, bf16[1024,1152]{1,0:T(8,128)(2,1)S(1)} %bitcast.84, bf16[1152,1152]{1,0:T(8,128)(2,1)} %stud_down.1, bf16[1024,1152]{1,0:T(8,128)(2,1)} %bitcast.88, s32[]{:T(128)S(6)} %select_n.32), kind=kOutput, calls=%fused_computation.32 | convolution fusion | flops 3080060928 | bytes 10919940 | tf_op jit(solution)/shard_map/dot_general | solution.py:584
  263.8 4.0 %fusion.23 = f32[144,1152]{1,0:T(8,128)} fusion(bf16[1024,1152]{1,0:T(8,128)(2,1)S(1)} %bitcast.85, f32[1024,1152]{1,0:T(8,128)} %get-tuple-element.60, s32[]{:T(128)S(6)} %select_n.32, f32[1024,1152]{1,0:T(8,128)} %get-tuple-element.61), kind=kOutput, calls=%fused_computation.44 | convolution fusion | flops 340033536 | bytes 5120004 | tf_op jit(solution)/shard_map/dot_general | solution.py:587
  (40 shorter events, 0.2 us)
Async XLA Ops:
  15.4 2.9 %copy-start.3 = (bf16[8,16,1152]{2,1,0:T(8,128)(2,1)}, bf16[8,16,1152]{2,1,0:T(8,128)(2,1)S(1)}, u32[]{:S(2)}) copy-start(bf16[8,16,1152]{2,1,0:T(8,128)(2,1)S(1)} %get-tuple-element.56) | copy-start | bytes 884740
  15.7 204.6 %copy-start.7 = (bf16[1001,1152]{1,0:T(8,128)(2,1)S(1)}, bf16[1001,1152]{1,0:T(8,128)(2,1)}, u32[]{:S(2)}) copy-start(bf16[1001,1152]{1,0:T(8,128)(2,1)} %param.24) | copy-start | bytes 6918916
  18.3 203.6 %copy-start.15 = (f32[1152]{0:T(1024)S(1)}, f32[1152]{0:T(1024)}, u32[]{:S(2)}) copy-start(f32[1152]{0:T(1024)} %param.35) | copy-start | bytes 13828
  18.3 205.6 %copy-start.13 = (f32[3,1152]{1,0:T(4,128)S(1)}, f32[3,1152]{1,0:T(4,128)}, u32[]{:S(2)}) copy-start(f32[3,1152]{1,0:T(4,128)} %param.34) | copy-start | bytes 41476
  18.3 205.6 %copy-start.14 = (f32[3,1152]{1,0:T(4,128)S(1)}, f32[3,1152]{1,0:T(4,128)}, u32[]{:S(2)}) copy-start(f32[3,1152]{1,0:T(4,128)} %param.33) | copy-start | bytes 41476
  216.2 8.7 %copy-start.8 = (bf16[16,1152]{1,0:T(8,128)(2,1)S(1)}, bf16[16,1152]{1,0:T(8,128)(2,1)}, u32[]{:S(2)}) copy-start(bf16[16,1152]{1,0:T(8,128)(2,1)} %embed_in.1) | copy-start | bytes 110596
  223.3 1.5 copy-start.10
  224.8 5.7 %copy-start = (bf16[8,128,1152]{2,1,0:T(8,128)(2,1)S(1)}, bf16[8,128,1152]{2,1,0:T(8,128)(2,1)}, u32[]{:S(2)}) copy-start(bf16[8,128,1152]{2,1,0:T(8,128)(2,1)} %get-tuple-element.9) | copy-start | bytes 7077892
  230.4 1.2 copy-start.11
  230.4 1.2 copy-start.9
  236.2 4.9 %copy-start.12 = (f32[64,16]{1,0:T(8,128)S(1)}, f32[64,16]{1,0:T(8,128)}, u32[]{:S(2)}) copy-start(f32[64,16]{1,0:T(8,128)} %copy-done.11) | copy-start | bytes 12292
  236.2 5.0 %copy-start.1 = (bf16[8,128,1152]{2,1,0:T(8,128)(2,1)S(1)}, bf16[8,128,1152]{2,1,0:T(8,128)(2,1)}, u32[]{:S(2)}) copy-start(bf16[8,128,1152]{2,1,0:T(8,128)(2,1)} %get-tuple-element.9) | copy-start | bytes 7077892
  241.2 2.8 %copy-start.6 = (f32[64,1152]{1,0:T(8,128)S(1)}, f32[64,1152]{1,0:T(8,128)}, u32[]{:S(2)}) copy-start(f32[64,1152]{1,0:T(8,128)} %get-tuple-element.27) | copy-start | bytes 884740
  244.0 4.2 %copy-start.4 = (bf16[1152,1152]{1,0:T(8,128)(2,1)S(1)}, bf16[1152,1152]{1,0:T(8,128)(2,1)}, u32[]{:S(2)}) copy-start(bf16[1152,1152]{1,0:T(8,128)(2,1)} %stud_up.1) | copy-start | bytes 7962628
  248.3 6.0 %copy-start.5 = (bf16[64,16,1152]{2,1,0:T(8,128)(2,1)}, bf16[64,16,1152]{2,1,0:T(8,128)(2,1)S(1)}, u32[]{:S(2)}) copy-start(bf16[64,16,1152]{2,1,0:T(8,128)(2,1)S(1)} %get-tuple-element.24) | copy-start | bytes 7077892
  248.3 6.0 %copy-start.2 = (bf16[64,16,1152]{2,1,0:T(8,128)(2,1)S(1)}, bf16[64,16,1152]{2,1,0:T(8,128)(2,1)}, u32[]{:S(2)}) copy-start(bf16[64,16,1152]{2,1,0:T(8,128)(2,1)} %get-tuple-element.23) | copy-start | bytes 7077892
where the time goes:
time: 269 us; the launch traced here: 268 us
  Pallas kernels  198 us (74%)
  matrix products  28.9 us (11%)
  other arithmetic  26.5 us (10%)
  local copies, waits for them, and re-layouts  13.5 us (5%)
    pallas_call x1, Pallas kernels, teacher_call(): pl.pallas_call(functools.partial(teacher_kernel, dims), out_shape=(jax.Sh...  198 us
    dot_general x1, matrix products, student_grads(): lax.dot_general(normed_share, back_pre, contract_rows, preferred_element_...  9.48 us
    dot_general x1, matrix products, student_front(): pre_act = jnp.dot(normed, student_up, preferred_element_type=jnp.float32)  6.01 us

commit v1 on v0

v1 whole, which is shorter than its diff:
```python
import functools
import math

import jax
import jax.numpy as jnp
import numpy as np
from jax import lax
from jax.experimental import pallas as pl
from jax.experimental.pallas import tpu as pltpu
from jax.sharding import PartitionSpec as P

CH = 16
TSTEPS = 1000
STRIDE = 125


norm_eps = 1e-06


def shifted(shard, axis, by):
    length = lax.axis_size(axis)
    return lax.ppermute(shard, axis, [(i, (i + by) % length) for i in range(length)])


def from_root(shard, axis, root):
    mine = lax.axis_index(axis) == root
    return lax.psum(jnp.where(mine, shard, jnp.zeros_like(shard)), axis)


def layer_norm(values):
    center = values - jnp.mean(values, axis=-1, keepdims=True)
    spread = jnp.mean(center * center, axis=-1, keepdims=True)
    return center * lax.rsqrt(spread + norm_eps)


def sinusoid(step_ids, model_width):
    half_width = model_width // 2
    frequency = jnp.exp(-math.log(10000.0) * jnp.arange(half_width, dtype=jnp.float32) / half_width)
    phase_arg = step_ids.astype(jnp.float32)[:, None] * frequency[None, :]
    return jnp.concatenate([jnp.cos(phase_arg), jnp.sin(phase_arg)], axis=-1)


def plan(step_ids):
    angle_t = 0.5 * math.pi / TSTEPS * step_ids.astype(jnp.float32)
    return (jnp.cos(angle_t), jnp.sin(angle_t))


def embed_tokens(latent, embed_in):
    leading = latent.shape[0]
    patches = latent.reshape(leading * (latent.shape[1] // CH), CH).astype(jnp.bfloat16)
    tokens = jnp.dot(patches, embed_in, preferred_element_type=jnp.float32)
    return tokens.reshape(leading, latent.shape[1] // CH, embed_in.shape[1]).astype(jnp.bfloat16)


def mlp_block(inputs, modulation, up_proj, down_proj):
    groups, seq_len, model_width = inputs.shape
    residual_in = inputs.astype(jnp.float32)
    shift_rows = modulation[:, 0, None, :]
    scale_rows = modulation[:, 1, None, :]
    gate_rows = modulation[:, 2, None, :]
    normed = (layer_norm(residual_in) * (1.0 + scale_rows) + shift_rows).astype(jnp.bfloat16)
    pre_act = jnp.dot(
        normed.reshape(groups * seq_len, model_width), up_proj, preferred_element_type=jnp.float32
    )
    hidden = jax.nn.gelu(pre_act, approximate=True).astype(jnp.bfloat16)
    mixed = jnp.dot(hidden, down_proj, preferred_element_type=jnp.float32).reshape(
        groups, seq_len, model_width
    )
    return (residual_in + gate_rows * mixed).astype(jnp.bfloat16)


def velocity(states, embed_out):
    groups, seq_len, model_width = states.shape
    normed = layer_norm(states.astype(jnp.float32)).astype(jnp.bfloat16)
    result = jnp.dot(
        normed.reshape(groups * seq_len, model_width), embed_out, preferred_element_type=jnp.float32
    )
    return result.reshape(groups, seq_len * embed_out.shape[1])


def ddim_step(latent, predicted, time_now, time_next):
    alpha_now, sigma_now = plan(time_now)
    alpha_next, sigma_next = plan(time_next)
    clean_est = alpha_now[:, None] * latent - sigma_now[:, None] * predicted
    noise_est = sigma_now[:, None] * latent + alpha_now[:, None] * predicted
    return alpha_next[:, None] * clean_est + sigma_next[:, None] * noise_est


def gelu_slope(pre_act):
    return jax.vjp(lambda inner: jax.nn.gelu(inner, approximate=True), pre_act)[1](
        jnp.ones_like(pre_act)
    )[0]


def run_chunks(count, one, operands, shared):
    if count == 1:
        return one(operands, *shared)

    def step(carry, piece):
        out = one(piece, *shared)
        return (carry[0] + out[0], carry[1] + out[1]), None

    split = [a.reshape((count, a.shape[0] // count) + a.shape[1:]) for a in operands]
    shapes = jax.eval_shape(one, [a[0] for a in split], *shared)
    zeros = tuple(jnp.zeros(s.shape, s.dtype) for s in shapes)
    return lax.scan(step, zeros, split)[0]


def teacher_chain(first_in, noised, guidance, step_index, mods, up, down, embed_in, embed_out):
    section_count = lax.axis_size("section")
    section_at = lax.axis_index("section")
    micro, seq_len, model_width = first_in.shape

    def paired(tokens):
        return jnp.broadcast_to(tokens[:, None], (micro, 2, seq_len, model_width)).reshape(
            2 * micro, seq_len, model_width
        )

    latent = noised
    states = paired(first_in)
    for which_step in range(2):
        mod = mods[which_step].reshape(2 * micro, 3, model_width)
        if which_step:
            states = paired(embed_tokens(latent, embed_in))
        for layer in range(section_count):
            states = mlp_block(states, mod, up, down)
            if layer < section_count - 1:
                states = lax.ppermute(states, "section", [(layer, layer + 1)])
        predicted = velocity(states, embed_out).reshape(micro, 2, -1)
        weight = guidance[:, None]
        guided = (1.0 + weight) * predicted[:, 0] - weight * predicted[:, 1]
        time_now = step_index - which_step * STRIDE
        stepped = ddim_step(latent, guided, time_now, time_now - STRIDE)
        if which_step == 0:
            returned = lax.ppermute(
                stepped, "section", [(section_count - 1, 0)]
            )
            latent = jnp.where(section_at == section_count - 1, stepped, returned)
    return stepped


def cos_of(angle, shift_quarter):
    quarters = jnp.floor(angle * (2.0 / math.pi) + 0.5)
    rest = ((angle - quarters * 1.5703125) - quarters * 4.837512969970703125e-4) - (
        quarters * 7.549789954891882e-8
    )
    turn = quarters - shift_quarter
    turn = turn - 4.0 * jnp.floor(turn * 0.25)
    square = rest * rest
    sine = rest + rest * square * (
        -1.6666654611e-1 + square * (8.3321608736e-3 - 1.9515295891e-4 * square)
    )
    cosine = (
        1.0
        - 0.5 * square
        + square
        * square
        * (4.166664568298827e-2 + square * (-1.388731625493765e-3 + 2.443315711809948e-5 * square))
    )
    odd = (turn == 1.0) | (turn == 3.0)
    negative = (turn == 1.0) | (turn == 2.0)
    value = jnp.where(odd, sine, cosine)
    return jnp.where(negative, -value, value)


NT = (((1,), (1,)), ((), ()))
GELU_A = math.sqrt(2.0 / math.pi)
GELU_B = 0.044715


def dot32(a, b, dims=(((1,), (0,)), ((), ()))):
    return lax.dot_general(a, b, dims, preferred_element_type=jnp.float32)


def gelu_pair(pre):
    square = pre * pre
    bent = jnp.tanh(GELU_A * (pre + GELU_B * square * pre))
    half = 0.5 * (1.0 + bent)
    slope = half + 0.5 * pre * (1.0 - bent * bent) * (GELU_A * (1.0 + 3.0 * GELU_B * square))
    return pre * half, slope


def token_mask(first, count, shape):
    lane = lax.broadcasted_iota(jnp.int32, shape, 1) // CH
    return [lane == first + k for k in range(count)]


def spread(values, first, count):
    masks = token_mask(first, count, values.shape)
    zero = jnp.zeros_like(values)
    return jnp.concatenate([jnp.where(m, values, zero) for m in masks], axis=0)


def gathered_tokens(values, first, count, rows):
    masks = token_mask(first, count, (rows, values.shape[1]))
    total = jnp.zeros((rows, values.shape[1]), jnp.float32)
    for k in range(count):
        total = total + jnp.where(masks[k], values[k * rows : (k + 1) * rows], 0.0)
    return total


def mega_kernel(
    dims,
    steps_in, labels_in, levels_in, clean_in, noise_in, up_shard, down_shard, t_gain, t_bias, s_gain, s_bias, guide_vec, freq,
    embed_in, embed_out_t, stud_up_hbm, stud_down_hbm, table_hbm,
    target_out, grad_up, grad_down,
    stud_up, stud_down, table, packed, up, down, tiled_in, tiled_out,
    noised, cols, wave, labs, scond, tok, slope, n_share, h_share, parts, pair_in, pair_sum,
    cross_in, mixed, xhat, rstd, pred, states, outs, latents, velo, target_all, hid,
    local_sem, send, recv, move_send, move_recv, z_send, z_recv, t_send, t_recv,
):
    sections, dps, micro, seq_len = dims
    total = dps * micro
    width = clean_in.shape[1]
    model = embed_in.shape[1]
    sec = lax.axis_index("section")
    me = lax.axis_index("dp")
    z, y = me // 2, me % 2
    core, side = sec % 2, z // 2
    tail = sections - 1
    mid_z, end_z, far_mid_z = 1 + side, 3 * side, 2 - side
    far_end_z = 3 - end_z
    is_mid = z == mid_z
    is_end = z == end_z
    oy = 1 - y
    E_y, E_o = end_z * 2 + y, end_z * 2 + oy
    A_y, A_o = mid_z * 2 + y, mid_z * 2 + oy
    B_y, B_o = far_mid_z * 2 + y, far_mid_z * 2 + oy
    F_y, F_o = far_end_z * 2 + y, far_end_z * 2 + oy
    MESH = pl.DeviceIdType.MESH
    devices = sections * dps
    mine = sec * dps + me

    barrier = pltpu.get_barrier_semaphore()

    def greet(k, carry):
        other = lax.rem(mine + k, devices)
        pl.semaphore_signal(
            barrier, inc=1, device_id={"section": other // dps, "dp": lax.rem(other, dps)},
            device_id_type=MESH,
        )
        return carry

    def place(who):
        zz, yy = who // 2, who % 2
        return (zz % 2) * (dps // 2) + (zz // 2) * 2 + yy

    lax.fori_loop(1, devices, greet, 0)
    row = lax.broadcasted_iota(jnp.int32, (micro, 128), 0)
    column = lax.broadcasted_iota(jnp.int32, (micro, 128), 1)
    cells = jnp.zeros((micro, 128), jnp.float32)
    for k, ref in enumerate((steps_in, labels_in, levels_in)):
        for b in range(micro):
            cells = jnp.where((row == b) & (column == k), ref[b].astype(jnp.float32), cells)
    slot = place(me)
    packed[slot, :, 0:width] = clean_in[...]
    packed[slot, :, width : 2 * width] = noise_in[...]
    packed[slot, :, 2 * width :] = cells
    locals_ = [
        pltpu.make_async_copy(stud_up_hbm, stud_up, local_sem.at[0]),
        pltpu.make_async_copy(stud_down_hbm, stud_down, local_sem.at[1]),
        pltpu.make_async_copy(table_hbm, table, local_sem.at[2]),
    ]
    for c in locals_:
        c.start()
    pl.semaphore_wait(barrier, devices - 1)

    def copy(i, src, dst, **device):
        return pltpu.make_async_remote_copy(
            src_ref=src, dst_ref=dst, send_sem=send.at[i], recv_sem=recv.at[i],
            device_id=device, device_id_type=MESH,
        )

    ur, dr = up_shard.shape[0], down_shard.shape[0]

    def urow(who):
        return up.at[pl.ds(pl.multiple_of(who * ur, 16), ur)]

    def drow(who, lo=0, n=None):
        return down.at[pl.ds(pl.multiple_of(who * dr + lo, 16), dr if n is None else n)]

    packs = [
        copy(k - 1, packed.at[slot], packed.at[slot], dp=lax.rem(me + k, dps))
        for k in range(1, dps)
    ]
    for c in packs:
        c.start()
    base = dps - 1
    names = [
        "ey_u", "ey_d", "ez_u", "ez_d", "ezo_u", "ezo_d", "det1", "det2", "det3",
        "ay_u", "ay_d", "am_u", "am_d", "ame_u", "ame_d", "amo",
        "ayf_u", "ayf_d", "aye_u", "aye_d", "pair", "cross", "back",
    ]
    index = {n: base + k for k, n in enumerate(names)}
    cut = (2 * dr // 3) // 16 * 16
    low, high = (0, cut), (cut, dr - cut)
    span = {"det1": low, "det2": low, "det3": low, "amo": low, "ay_d": high, "aye_d": high}

    def own(name, dst):
        if name.endswith("u"):
            return copy(index[name], up_shard, urow(me), dp=dst)
        lo, n = span.get(name, (0, dr))
        return copy(index[name], down_shard.at[pl.ds(lo, n)], drow(me, lo, n), dp=dst)

    def piece(name, who, dst):
        ref = urow(who) if name.endswith("u") else drow(who, *span.get(name, (0, dr)))
        return copy(index[name], ref, ref, dp=dst)

    end_sends = (("ez_u", A_y), ("ey_u", E_o), ("ez_d", A_y), ("ey_d", E_o))
    mid_sends = (
        ("am_u", B_y), ("ay_u", A_o), ("det1", E_y), ("am_d", B_y), ("ay_d", A_o)
    )

    @pl.when(is_end)
    def _():
        for n, dst in end_sends:
            own(n, dst).start()

    @pl.when(is_mid)
    def _():
        for n, dst in mid_sends:
            own(n, dst).start()
        up[pl.ds(pl.multiple_of(me * ur, 16), ur)] = up_shard[...]
        down[pl.ds(pl.multiple_of(me * dr, 16), dr)] = down_shard[...]

    def relay(part):
        @pl.when(is_end)
        def _():
            piece("ey_" + part, E_o, E_o).wait_recv()
            piece("ezo_" + part, E_o, A_y).start()
            if part == "u":
                piece("det1", A_y, E_o).wait_recv()
                piece("det2", A_y, E_o).start()
            else:
                piece("det2", A_o, A_y).wait_recv()
                piece("det3", A_o, A_y).start()

        @pl.when(is_mid)
        def _():
            piece("ez_" + part, E_y, B_y).wait_recv()
            piece("ame_" + part, E_y, B_y).start()
            piece("am_" + part, B_y, A_o).wait_recv()
            piece("ayf_" + part, B_y, A_o).start()

    for k in range(seq_len):
        tiled_in[k * CH : (k + 1) * CH] = embed_in[...]
        tiled_out[k * CH : (k + 1) * CH] = embed_out_t[...]
    lane_model = lax.broadcasted_iota(jnp.int32, (1, model), 1)
    sine_lane = jnp.where(lane_model >= model // 2, 1.0, 0.0)
    for c in packs:
        c.wait_recv()
    data = packed[...].reshape(total, packed.shape[2])
    steps = data[:, 2 * width : 2 * width + 1]
    label = data[:, 2 * width + 1 : 2 * width + 2]
    guide = 0.5 * data[:, 2 * width + 2 : 2 * width + 3]
    for k in range(3):
        angle = jnp.broadcast_to(
            (0.5 * math.pi / TSTEPS) * (steps - float(k * STRIDE)), (total, 128)
        )
        cols[2 * k] = cos_of(angle, 0.0)
        cols[2 * k + 1] = cos_of(angle, 1.0)
    cols[6] = jnp.broadcast_to(guide, (total, 128))
    alpha_t, sigma_t = cols[0][:, 0:1], cols[1][:, 0:1]
    clean = alpha_t * data[:, :width] + sigma_t * data[:, width : 2 * width]
    noised[...] = clean
    for k in range(2):
        wave[k] = cos_of((steps - float(k * STRIDE)) * freq[...], sine_lane)
    for c in locals_:
        c.wait()
    classes = table.shape[0] - 1
    whole = (classes // 16) * 16
    ids = lax.broadcasted_iota(jnp.int32, (total, whole), 1).astype(jnp.float32)
    rows = dot32(jnp.where(ids == label, 1.0, 0.0).astype(jnp.bfloat16), table[:whole])
    rest = table[whole:].astype(jnp.float32)
    for k in range(classes - whole):
        rows = rows + jnp.where(label == float(whole + k), rest[k : k + 1], 0.0)
    labs[0] = rows
    labs[1] = jnp.broadcast_to(rest[classes - whole : classes - whole + 1], (total, model))
    scond[...] = wave[0] + rows + guide * guide_vec[...]

    block = seq_len // 2
    blocks = 4
    group = total // 2
    brows = block * group
    share = n_share.shape[0]
    pick = jnp.where(
        lax.broadcasted_iota(jnp.int32, (share, model), 1)
        == lax.broadcasted_iota(jnp.int32, (share, model), 0) + me * share,
        1.0, 0.0,
    ).astype(jnp.bfloat16)

    def at_block(i):
        return pl.ds(pl.multiple_of(i * brows, brows), brows)

    def members(i):
        return pl.ds(pl.multiple_of((i // 2) * group, group), group)

    def first_of(i):
        return lax.rem(i, 2) * block

    def student_part(i, k):
        return scond[members(i)] * s_gain[k : k + 1] + s_bias[k : k + 1]

    def front(i, carry):
        here = at_block(i)
        tokens = dot32(
            spread(noised[members(i)], first_of(i), block).astype(jnp.bfloat16), tiled_in[...]
        ).astype(jnp.bfloat16)
        tok[here] = tokens
        cube = layer_norm(tokens.astype(jnp.float32)).reshape(block, group, model)
        normed = (cube * (1.0 + student_part(i, 1))[None] + student_part(i, 0)[None]).astype(
            jnp.bfloat16
        )
        normed = normed.reshape(brows, model)
        n_share[:, here] = dot32(pick, normed, NT).astype(jnp.bfloat16)
        hidden, bend = gelu_pair(dot32(normed, stud_up[...]))
        hidden = hidden.astype(jnp.bfloat16)
        slope[here] = bend
        h_share[:, here] = dot32(pick, hidden, NT).astype(jnp.bfloat16)
        parts[here] = dot32(hidden, stud_down[...]).astype(jnp.bfloat16)
        return carry

    lax.fori_loop(0, blocks, front, 0)

    half_rows = seq_len * total // 2

    def half_of(ref, c):
        return ref.at[pl.ds(pl.multiple_of(c * half_rows, half_rows), half_rows)]

    sibling = sec + 1 - 2 * core
    pair = copy(index["pair"], half_of(parts, 1 - core), pair_in, section=sibling)
    cross = copy(index["cross"], pair_sum, cross_in, section=lax.rem(sec + 2, sections))
    back = copy(index["back"], half_of(mixed, core), half_of(mixed, core), section=sibling)
    pair.start()
    relay("u")
    pair.wait_recv()
    pair_sum[...] = (
        half_of(parts, core)[...].astype(jnp.float32) + pair_in[...].astype(jnp.float32)
    ).astype(jnp.bfloat16)
    cross.start()
    relay("d")
    turned = model // 4

    def turn(i, carry):
        here = pl.ds(pl.multiple_of(i * turned, turned), turned)
        eye = jnp.where(
            lax.broadcasted_iota(jnp.int32, (turned, model), 1)
            == lax.broadcasted_iota(jnp.int32, (turned, model), 0) + i * turned,
            1.0, 0.0,
        ).astype(jnp.bfloat16)
        stud_up[here] = dot32(eye, stud_down[...], NT).astype(jnp.bfloat16)
        return carry

    lax.fori_loop(0, 4, turn, 0)

    @pl.when(is_mid)
    def _():
        piece("ame_u", F_y, A_o).wait_recv()
        piece("aye_u", F_y, A_o).start()

    cross.wait_recv()
    mixed[pl.ds(pl.multiple_of(core * half_rows, half_rows), half_rows)] = (
        pair_sum[...].astype(jnp.float32) + cross_in[...].astype(jnp.float32)
    ).astype(jnp.bfloat16)
    back.start()

    @pl.when(is_mid)
    def _():
        piece("ezo_d", E_o, B_y).wait_recv()
        piece("amo", E_o, B_y).start()
        piece("ame_d", F_y, A_o).wait_recv()
        piece("aye_d", F_y, A_o).start()

    back.wait_recv()
    pred[...] = jnp.zeros_like(pred)

    def middle(i, carry):
        here = at_block(i)
        state = tok[here].astype(jnp.float32).reshape(block, group, model) + student_part(i, 2)[
            None
        ] * mixed[here].astype(jnp.float32).reshape(block, group, model)
        state = state.reshape(brows, model)
        center = state - jnp.mean(state, axis=-1, keepdims=True)
        inverse = lax.rsqrt(jnp.mean(center * center, axis=-1, keepdims=True) + norm_eps)
        unit = center * inverse
        xhat[here] = unit
        rstd[here] = jnp.broadcast_to(inverse, (brows, 128))
        pred[members(i)] += gathered_tokens(
            dot32(unit.astype(jnp.bfloat16), tiled_out[...], NT), first_of(i), block, group
        )
        return carry

    lax.fori_loop(0, blocks, middle, 0)

    trows = micro * seq_len
    chunk = 768 if up.shape[1] % 768 == 0 else up.shape[1]

    def owned(j):
        return j * (dps // 2) + (z - 1) * 2 + y

    def sample_rows(d):
        return pl.ds(pl.multiple_of(d * micro, micro), micro)

    def move(i):
        return pltpu.make_async_remote_copy(
            src_ref=outs.at[i], dst_ref=states.at[i],
            send_sem=move_send.at[i], recv_sem=move_recv.at[i],
            device_id={"section": lax.rem(sec + 1, sections)}, device_id_type=MESH,
        )

    def back_move(j):
        return pltpu.make_async_remote_copy(
            src_ref=latents.at[1, j], dst_ref=latents.at[1, j],
            send_sem=z_send.at[j], recv_sem=z_recv.at[j],
            device_id={"section": 0}, device_id_type=MESH,
        )

    def target_copy(k, j, d):
        other = lax.rem(mine + k, devices)
        return pltpu.make_async_remote_copy(
            src_ref=target_all.at[d], dst_ref=target_all.at[d],
            send_sem=t_send.at[j * devices + k], recv_sem=t_recv.at[d],
            device_id={"section": other // dps, "dp": lax.rem(other, dps)}, device_id_type=MESH,
        )

    @pl.when(is_mid)
    def _():
        for n, who in (
            ("ay_u", A_o), ("ay_d", A_o), ("det3", A_o), ("ayf_u", B_o), ("ayf_d", B_o),
            ("ezo_u", E_o), ("aye_u", F_o), ("aye_d", F_o), ("amo", F_o),
        ):
            piece(n, who, A_o).wait_recv()
        for j in range(2):
            latents[0, j] = noised[sample_rows(owned(j))]

        def task(i, carry):
            step, j, half = i // 4, lax.rem(i // 2, 2), lax.rem(i, 2)
            d = owned(j)
            here = sample_rows(d)

            @pl.when(sec == 0)
            def _():
                @pl.when((step == 1) & (half == 0))
                def _():
                    back_move(j).wait_recv()

                states[i] = dot32(
                    spread(latents[step, j], 0, seq_len).astype(jnp.bfloat16), tiled_in[...]
                ).astype(jnp.bfloat16)

            @pl.when(sec > 0)
            def _():
                move(i).wait_recv()

            cond = wave[step, here] + labs[half, here]
            residual = states[i].astype(jnp.float32)
            cube = layer_norm(residual).reshape(seq_len, micro, model)
            scale = cond * t_gain[1] + t_bias[1]
            shift = cond * t_gain[0] + t_bias[0]
            gate = cond * t_gain[2] + t_bias[2]
            normed = (cube * (1.0 + scale)[None] + shift[None]).astype(jnp.bfloat16)
            normed = normed.reshape(trows, model)
            for k in range(up.shape[1] // chunk):
                hid[:, k * chunk : (k + 1) * chunk] = jax.nn.gelu(
                    dot32(normed, up[:, k * chunk : (k + 1) * chunk]), approximate=True
                ).astype(jnp.bfloat16)
            acc = dot32(hid[...], down[...])
            out = residual.reshape(seq_len, micro, model) + gate[None] * acc.reshape(
                seq_len, micro, model
            )
            outs[i] = out.reshape(trows, model).astype(jnp.bfloat16)

            @pl.when(sec < tail)
            def _():
                move(i).start()

            @pl.when(sec == tail)
            def _():
                last = layer_norm(outs[i].astype(jnp.float32)).astype(jnp.bfloat16)
                velo[half] = gathered_tokens(
                    dot32(last, tiled_out[...], NT), 0, seq_len, micro
                )

                @pl.when(half == 1)
                def _():
                    level = cols[6, here][:, 0:1]
                    guided = (1.0 + level) * velo[0] - level * velo[1]
                    a_now = cols[2 * step, here][:, 0:1]
                    s_now = cols[2 * step + 1, here][:, 0:1]
                    a_next = cols[2 * step + 2, here][:, 0:1]
                    s_next = cols[2 * step + 3, here][:, 0:1]
                    before = latents[step, j]
                    after = a_next * (a_now * before - s_now * guided) + s_next * (
                        s_now * before + a_now * guided
                    )

                    @pl.when(step == 0)
                    def _():
                        latents[1, j] = after
                        back_move(j).start()

                    @pl.when(step == 1)
                    def _():
                        a_first, s_first = cols[0, here][:, 0:1], cols[1, here][:, 0:1]
                        ratio = s_next / s_first
                        target_all[d] = (after - ratio * latents[0, j]) / (a_next - ratio * a_first)

                        def tell(k, carry):
                            target_copy(k, j, d).start()
                            return carry

                        lax.fori_loop(1, devices, tell, 0)

            return carry

        lax.fori_loop(0, 8, task, 0)

    grad_up[...] = jnp.zeros_like(grad_up)
    grad_down[...] = jnp.zeros_like(grad_down)

    def finish(i, carry):
        here = at_block(i)
        slopes = dot32(
            spread(pred[members(i)], first_of(i), block).astype(jnp.bfloat16), tiled_out[...]
        ) + dot32(
            spread(noised[members(i)], first_of(i), block).astype(jnp.bfloat16), tiled_out[...]
        )
        unit = xhat[here]
        mean = jnp.mean(slopes, axis=-1, keepdims=True)
        along = jnp.mean(slopes * unit, axis=-1, keepdims=True)
        back_state = rstd[here][:, 0:1] * (slopes - mean - unit * along)
        back_part = (student_part(i, 2)[None] * back_state.reshape(block, group, model)).astype(
            jnp.bfloat16
        ).reshape(brows, model)
        grad_down[...] += dot32(h_share[:, here], back_part)
        back_pre = (dot32(back_part, stud_up[...]) * slope[here]).astype(jnp.bfloat16)
        grad_up[...] += dot32(n_share[:, here], back_pre)
        return carry

    for part in range(2):
        for k in range(dps // 2):
            d = part * (dps // 2) + k

            @pl.when(jnp.logical_not((sec == tail) & (z == 1 + k // 2) & (y == k % 2)))
            def _():
                target_copy(1, 0, d).wait_recv()

        these = pl.ds(part * group, group)
        alpha_h, sigma_h = cols[0, these][:, 0:1], cols[1, these][:, 0:1]
        weight = jnp.maximum(alpha_h * alpha_h / (sigma_h * sigma_h), 1.0)
        estimate = alpha_h * noised[these] - sigma_h * pred[these]
        goal = target_all[pl.ds(part * (dps // 2), dps // 2)].reshape(group, width)
        seed = (-2.0 / (total * width)) * (sigma_h * weight) * (estimate - goal)
        seed_hi = seed.astype(jnp.bfloat16).astype(jnp.float32)
        pred[these] = seed_hi
        noised[these] = seed - seed_hi
        lax.fori_loop(2 * part, 2 * part + 2, finish, 0)

    target_out[...] = target_all[slot]

    for c in packs + [pair, cross, back]:
        c.wait_send()

    @pl.when(is_end)
    def _():
        for n, dst in end_sends:
            own(n, dst).wait_send()
        for n, who, dst in (
            ("ezo_u", E_o, A_y), ("ezo_d", E_o, A_y), ("det2", A_y, E_o), ("det3", A_o, A_y)
        ):
            piece(n, who, dst).wait_send()

    @pl.when(is_mid)
    def _():
        for n, dst in mid_sends:
            own(n, dst).wait_send()
        for n, who, dst in (
            ("ame_u", E_y, B_y), ("ame_d", E_y, B_y), ("amo", E_o, B_y),
            ("ayf_u", B_y, A_o), ("ayf_d", B_y, A_o), ("aye_u", F_y, A_o), ("aye_d", F_y, A_o),
        ):
            piece(n, who, dst).wait_send()

        @pl.when(sec < tail)
        def _():
            def done(i, carry):
                move(i).wait_send()
                return carry

            lax.fori_loop(0, 8, done, 0)

        @pl.when(sec == tail)
        def _():
            for j in range(2):
                back_move(j).wait_send()

                def told(k, carry):
                    target_copy(k, j, owned(j)).wait_send()
                    return carry

                lax.fori_loop(1, devices, told, 0)


def flush_kernel(a, b, c, x, y, z):
    x[...] = a[...]
    y[...] = b[...]
    z[...] = c[...]


def mega_call(dims, operands):
    sections, dps, micro, seq_len = dims
    clean, up_shard, down_shard = operands[3], operands[5], operands[6]
    hidden, model = up_shard.shape[1], down_shard.shape[1]
    stud_up, stud_down, table = operands[-3:]
    width = clean.shape[1]
    total = dps * micro
    rows = total * seq_len
    trows = micro * seq_len
    share_up, share_down = model // dps, stud_down.shape[0] // dps
    f32, bf16 = jnp.float32, jnp.bfloat16
    vmem = pl.BlockSpec(memory_space=pltpu.VMEM)
    hbm = pl.BlockSpec(memory_space=pl.ANY)
    smem = pl.BlockSpec(memory_space=pltpu.SMEM)
    V, D = pltpu.VMEM, pltpu.SemaphoreType.DMA
    results = pl.pallas_call(
        functools.partial(mega_kernel, dims),
        out_shape=(
            jax.ShapeDtypeStruct((micro, width), f32),
            jax.ShapeDtypeStruct((share_up, stud_up.shape[1]), f32),
            jax.ShapeDtypeStruct((share_down, model), f32),
        ),
        in_specs=[smem] * 3 + [vmem] * (len(operands) - 6) + [hbm] * 3,
        out_specs=(vmem,) * 3,
        scratch_shapes=[
            V(stud_up.shape, bf16), V(stud_down.shape, bf16), V(table.shape, bf16),
            V((dps, micro, 2 * width + 128), f32),
            V((up_shard.shape[0] * dps, hidden), bf16),
            V((down_shard.shape[0] * dps, model), bf16),
            V((width, model), bf16), V((width, model), bf16),
            V((total, width), f32), V((7, total, 128), f32),
            V((2, total, model), f32), V((2, total, model), f32), V((total, model), f32),
            V((rows, model), bf16), V((rows, model), f32),
            V((share_up, rows), bf16), V((share_down, rows), bf16),
            V((rows, model), bf16), V((rows // 2, model), bf16), V((rows // 2, model), bf16),
            V((rows // 2, model), bf16), V((rows, model), bf16),
            V((rows, model), f32), V((rows, 128), f32), V((total, width), f32),
            V((8, trows, model), bf16), V((8, trows, model), bf16),
            V((2, 2, micro, width), f32), V((2, micro, width), f32), V((dps, micro, width), f32),
            V((trows, hidden), bf16),
            D((3,)), D((32,)), D((32,)), D((8,)), D((8,)), D((2,)), D((2,)),
            D((2 * sections * dps,)), D((dps,)),
        ],
        compiler_params=pltpu.CompilerParams(
            collective_id=0, has_side_effects=True, vmem_limit_bytes=63 << 20
        ),
    )(*operands)
    return pl.pallas_call(
        flush_kernel,
        out_shape=tuple(jax.ShapeDtypeStruct(r.shape, r.dtype) for r in results),
        in_specs=[vmem] * 3,
        out_specs=(vmem,) * 3,
    )(*results)


def body(
    clean_latent,
    noise_draw,
    step_index,
    labels,
    guide_level,
    class_table,
    embed_in,
    embed_out,
    teacher_up,
    teacher_down,
    teacher_gain,
    teacher_bias,
    student_up,
    student_down,
    student_gain,
    student_bias,
    guide_vec,
):
    section_count = lax.axis_size("section")
    dp_count = lax.axis_size("dp")
    section_at = lax.axis_index("section")
    dp_at = lax.axis_index("dp")
    micro = clean_latent.shape[0]
    width = clean_latent.shape[1]
    seq_len = width // CH
    model_width = class_table.shape[1]
    fused = (
        dp_count == 8
        and section_count == 4
        and micro == 8
        and seq_len % 4 == 0
        and width % 128 == 0
        and teacher_up.shape[1] % 16 == 0
        and teacher_down.shape[1] % 16 == 0
        and student_up.shape[1] == student_down.shape[0] == model_width
    )
    if fused:
        half_width = model_width // 2
        frequency = np.exp(-math.log(10000.0) * np.arange(half_width) / half_width)
        frequency = np.tile(frequency, 2)[None].astype(np.float32)
        return mega_call(
            (section_count, dp_count, micro, seq_len),
            (
                step_index, labels, guide_level, clean_latent, noise_draw,
                teacher_up[0], teacher_down[0],
                teacher_gain.reshape(3, 1, model_width), teacher_bias.reshape(3, 1, model_width),
                student_gain, student_bias, guide_vec[None], jnp.asarray(frequency),
                embed_in, embed_out.T, student_up, student_down, class_table,
            ),
        )
    alpha_t, sigma_t = plan(step_index)
    noised = alpha_t[:, None] * clean_latent + sigma_t[:, None] * noise_draw
    guidance = 0.5 * guide_level.astype(jnp.float32)
    label_rows = jnp.take(class_table, labels, axis=0).astype(jnp.float32)
    null_row = class_table[class_table.shape[0] - 1].astype(jnp.float32)
    wave_rows = jnp.stack(
        [sinusoid(step_index - step_k * STRIDE, model_width) for step_k in range(2)]
    )
    conditions = jnp.stack(
        [wave_rows + label_rows[None], wave_rows + null_row[None, None, :]], axis=2
    )
    mods = (
        conditions[:, :, :, None, :] * teacher_gain[0][None, None, None]
        + teacher_bias[0][None, None, None]
    )
    first_in = embed_tokens(noised, embed_in)
    alpha_end, sigma_end = plan(step_index - 2 * STRIDE)
    sigma_ratio = sigma_end / sigma_t
    packed = jnp.concatenate(
        [
            noised,
            step_index.astype(jnp.float32)[:, None],
            labels.astype(jnp.float32)[:, None],
            guide_level.astype(jnp.float32)[:, None],
        ],
        axis=1,
    )
    def student_normed(noised, steps, labels, guidance):
        rows = noised.shape[0] * seq_len
        label_rows = jnp.take(class_table, labels, axis=0).astype(jnp.float32)
        cond = sinusoid(steps, model_width) + label_rows + guidance[:, None] * guide_vec[None, :]
        modulation = cond[:, None, :] * student_gain[None] + student_bias[None]
        residual_in = embed_tokens(noised, embed_in).astype(jnp.float32)
        normed = (
            (layer_norm(residual_in) * (1.0 + modulation[:, 1, None, :]) + modulation[:, 0, None, :])
            .astype(jnp.bfloat16)
            .reshape(rows, model_width)
        )
        return residual_in, modulation[:, 2, None, :], normed

    def student_front(noised, steps, labels, guidance, student_up):
        residual_in, gate_rows, normed = student_normed(noised, steps, labels, guidance)
        pre_act = jnp.dot(normed, student_up, preferred_element_type=jnp.float32)
        hidden = jax.nn.gelu(pre_act, approximate=True).astype(jnp.bfloat16)
        return residual_in, gate_rows, normed, pre_act, hidden

    total = micro * dp_count
    element_count = total * width
    up_share = model_width // dp_count
    down_share = student_down.shape[0] // dp_count

    goal_scale = 1.0 / (alpha_end - sigma_ratio * alpha_t)
    up = lax.all_gather(teacher_up[0], "dp", axis=0, tiled=True)
    down = lax.all_gather(teacher_down[0], "dp", axis=0, tiled=True)
    ending = teacher_chain(
        first_in, noised, guidance, step_index, mods, up, down, embed_in, embed_out
    )
    goal_latent = (ending - sigma_ratio[:, None] * noised) * goal_scale[:, None]
    packed = lax.all_gather(packed, "dp", axis=0, tiled=True)
    own = student_front(noised, step_index, labels, guidance, student_up)
    partial_value = jnp.dot(own[4], student_down, preferred_element_type=jnp.float32)
    mixed = lax.psum(partial_value.astype(jnp.bfloat16), "section")
    all_mixed = lax.all_gather(mixed, "dp", axis=0, tiled=True)
    gathered = lax.all_gather(goal_latent, ("section", "dp"), axis=0, tiled=True)
    all_target = gathered[total * (section_count - 1):]
    all_mixed = all_mixed.reshape(total, seq_len, model_width)
    all_noised = packed[:, :width]
    all_steps = packed[:, width].astype(jnp.int32)
    all_labels = packed[:, width + 1].astype(jnp.int32)
    all_guidance = 0.5 * packed[:, width + 2]
    distill_target = lax.dynamic_slice_in_dim(all_target, dp_at * micro, micro, 0)

    def student_grads(operands, student_up, student_down):
        noised, steps, labels, guidance, mixed, target = operands
        count = noised.shape[0]
        rows = count * seq_len
        residual_in, gate_rows, normed, pre_act, hidden = student_front(
            noised, steps, labels, guidance, student_up
        )
        state_rows = residual_in + gate_rows * mixed.astype(jnp.float32)
        alpha_t, sigma_t = plan(steps)
        normed_out, pullback = jax.vjp(layer_norm, state_rows)
        predicted = jnp.dot(
            normed_out.astype(jnp.bfloat16).reshape(rows, model_width),
            embed_out,
            preferred_element_type=jnp.float32,
        ).reshape(count, width)
        estimate = alpha_t[:, None] * noised - sigma_t[:, None] * predicted
        weight = jnp.maximum(alpha_t * alpha_t / (sigma_t * sigma_t), 1.0)
        slope_pred = -2.0 / element_count * (sigma_t * weight)[:, None] * (estimate - target)
        back_norm = jnp.dot(
            slope_pred.reshape(rows, CH),
            embed_out.astype(jnp.float32).T,
            precision=lax.Precision.HIGHEST,
        )
        back_state = pullback(back_norm.reshape(count, seq_len, model_width))[0]
        back_part = (gate_rows * back_state).astype(jnp.bfloat16).reshape(rows, model_width)
        back_hidden = lax.dot_general(
            back_part, student_down, (((1,), (1,)), ((), ())), preferred_element_type=jnp.float32
        )
        back_pre = (back_hidden * gelu_slope(pre_act)).astype(jnp.bfloat16)
        normed_share = lax.dynamic_slice_in_dim(normed, dp_at * up_share, up_share, 1)
        hidden_share = lax.dynamic_slice_in_dim(hidden, dp_at * down_share, down_share, 1)
        contract_rows = (((0,), (0,)), ((), ()))
        return (
            lax.dot_general(
                normed_share, back_pre, contract_rows, preferred_element_type=jnp.float32
            ),
            lax.dot_general(
                hidden_share, back_part, contract_rows, preferred_element_type=jnp.float32
            ),
        )

    operands = [all_noised, all_steps, all_labels, all_guidance, all_mixed, all_target]
    grad_up, grad_down = run_chunks(
        max(1, dp_count // 8), student_grads, operands, (student_up, student_down)
    )
    return (distill_target, grad_up, grad_down)


def solution(mesh):
    return jax.shard_map(
        body,
        mesh=mesh,
        in_specs=(
            P("dp", None),
            P("dp", None),
            P("dp"),
            P("dp"),
            P("dp"),
            P(),
            P(),
            P(),
            P("section", "dp", None),
            P("section", "dp", None),
            P("section", None, None),
            P("section", None, None),
            P(None, "section"),
            P("section", None),
            P(),
            P(),
            P(),
        ),
        out_specs=(P("dp", None), P("dp", "section"), P(("section", "dp"), None)),
        check_vma=False,
    )
```

time: 269 us -> 144 us (0.54)
  Pallas kernels: 198 us -> 141 us
  matrix products: 28.9 us -> 0 us
  other arithmetic: 26.5 us -> 0 us
  local copies, waits for them, and re-layouts: 13.5 us -> 1.29 us
    pallas_call x1 -> x2, Pallas kernels: 198 us -> 141 us  [the longest x1 139 us: mega_call(): pl.pallas_call(functools.partial(mega_kernel, dims), out_shape=(jax.Shape...]
    dot_general x7 -> x0, matrix products: 28.9 us -> none  [the longest x1 9.48 us: student_grads(): lax.dot_general(normed_share, back_pre, contract_rows, preferred_element_...]
    convert_element_type x7 -> x0, other arithmetic: 8.69 us -> none  [the longest x1 4.19 us: student_grads(): (gate_rows * back_state).astype(jnp.bfloat16).reshape(rows, model_width)]
    reduce_sum x3 -> x0, other arithmetic: 5.8 us -> none  [the longest x2 3.03 us: layer_norm(): spread = jnp.mean(center * center, axis=-1, keepdims=True)]
    gather x2 -> x0, local copies, waits for them, and re-layouts: 3.28 us -> none  [student_normed(): label_rows = jnp.take(class_table, labels, axis=0).astype(jnp.float32)]
    mul x5 -> x0, other arithmetic: 2.97 us -> none  [the longest x2 2.18 us: student_grads(): -2.0 / element_count * (sigma_t * weight)[:, None] * (estimate - target)]
where the time goes in v1:
time: 144 us; the launch traced here: 143 us
  Pallas kernels  141 us (98%)
    pallas_call x1, Pallas kernels, mega_call(): pl.pallas_call(functools.partial(mega_kernel, dims), out_shape=(jax.Shape...  139 us

profile of v1, /device:TPU:0, one launch (start us, length us, event | category | flops | bytes accessed | tf_op | source)
XLA Modules:
  0.0 143.3 jit_solution(14145884059143325746)
XLA Ops:
  0.6 1.3 broadcast_in_dim.3.guide_vec
  1.9 139.0 %shard_map.193 = (f32[8,256]{1,0:T(8,128)}, f32[144,1152]{1,0:T(8,128)}, f32[144,1152]{1,0:T(8,128)}) custom-call(s32[8]{0:T(128)} %steps_in.1, s32[8]{0:T(128)} %labels_in.1, s32[8]{0:T(128)} %levels_in.1, f32[8,256]{1,0:T(8,128)} %clean_in.1, f32[8,256]{1,0:T(8,128)} %noise_in.1, bf16[144,2304]{1,0:T(8,128)(2,1)} %bitcast.5, bf16[288,1152]{1,0:T(8,128)(2,1)} %bitcast.6, ...), custom_call_target="tpu_custom_call" | custom-call | tf_op jit(solution)/shard_map/pallas_call | solution.py:724
  140.9 2.4 %shard_map.194 = (f32[8,256]{1,0:T(8,128)}, f32[144,1152]{1,0:T(8,128)}, f32[144,1152]{1,0:T(8,128)}) custom-call(f32[8,256]{1,0:T(8,128)} %get-tuple-element.6.a, f32[144,1152]{1,0:T(8,128)} %get-tuple-element.7.b, f32[144,1152]{1,0:T(8,128)} %get-tuple-element.8.c), custom_call_target="tpu_custom_call" | custom-call | tf_op jit(solution)/shard_map/pallas_call | solution.py:756

commit v2 on v1

--- a/solution.py
+++ b/solution.py
@@ -207,7 +207,7 @@
     stud_up, stud_down, table, packed, up, down, tiled_in, tiled_out,
     noised, cols, wave, labs, scond, tok, slope, n_share, h_share, parts, pair_in, pair_sum,
     cross_in, mixed, xhat, rstd, pred, states, outs, latents, velo, target_all, hid,
-    local_sem, send, recv, move_send, move_recv, z_send, z_recv, t_send, t_recv,
+    local_sem, send, recv, move_send, move_recv, z_send, z_recv, t_send, t_recv, gate,
 ):
     sections, dps, micro, seq_len = dims
     total = dps * micro
@@ -261,7 +261,19 @@
         pltpu.make_async_copy(stud_down_hbm, stud_down, local_sem.at[1]),
         pltpu.make_async_copy(table_hbm, table, local_sem.at[2]),
     ]
-    for c in locals_:
+    ur, dr = up_shard.shape[0], down_shard.shape[0]
+
+    def urow(who):
+        return up.at[pl.ds(pl.multiple_of(who * ur, 16), ur)]
+
+    def drow(who, lo=0, n=None):
+        return down.at[pl.ds(pl.multiple_of(who * dr + lo, 16), dr if n is None else n)]
+
+    shards = [
+        pltpu.make_async_copy(up_shard, urow(me), local_sem.at[3]),
+        pltpu.make_async_copy(down_shard, drow(me), local_sem.at[4]),
+    ]
+    for c in shards + locals_:
         c.start()
     pl.semaphore_wait(barrier, devices - 1)
 
@@ -270,14 +282,6 @@
             src_ref=src, dst_ref=dst, send_sem=send.at[i], recv_sem=recv.at[i],
             device_id=device, device_id_type=MESH,
         )
-
-    ur, dr = up_shard.shape[0], down_shard.shape[0]
-
-    def urow(who):
-        return up.at[pl.ds(pl.multiple_of(who * ur, 16), ur)]
-
-    def drow(who, lo=0, n=None):
-        return down.at[pl.ds(pl.multiple_of(who * dr + lo, 16), dr if n is None else n)]
 
     packs = [
         copy(k - 1, packed.at[slot], packed.at[slot], dp=lax.rem(me + k, dps))
@@ -287,20 +291,14 @@
         c.start()
     base = dps - 1
     names = [
-        "ey_u", "ey_d", "ez_u", "ez_d", "ezo_u", "ezo_d", "det1", "det2", "det3",
+        "ey_u", "ey_d", "ez_u", "ez_d", "ezo_u", "ezo_d", "ezo_r", "det1", "det2", "det3",
         "ay_u", "ay_d", "am_u", "am_d", "ame_u", "ame_d", "amo",
         "ayf_u", "ayf_d", "aye_u", "aye_d", "pair", "cross", "back",
     ]
     index = {n: base + k for k, n in enumerate(names)}
     cut = (2 * dr // 3) // 16 * 16
     low, high = (0, cut), (cut, dr - cut)
-    span = {"det1": low, "det2": low, "det3": low, "amo": low, "ay_d": high, "aye_d": high}
-
-    def own(name, dst):
-        if name.endswith("u"):
-            return copy(index[name], up_shard, urow(me), dp=dst)
-        lo, n = span.get(name, (0, dr))
-        return copy(index[name], down_shard.at[pl.ds(lo, n)], drow(me, lo, n), dp=dst)
+    span = {"ezo_d": low, "ezo_r": high, "det1": low, "det2": low, "det3": low, "amo": low, "ay_d": high, "aye_d": high}
 
     def piece(name, who, dst):
         ref = urow(who) if name.endswith("u") else drow(who, *span.get(name, (0, dr)))
@@ -311,23 +309,24 @@
         ("am_u", B_y), ("ay_u", A_o), ("det1", E_y), ("am_d", B_y), ("ay_d", A_o)
     )
 
-    @pl.when(is_end)
-    def _():
-        for n, dst in end_sends:
-            own(n, dst).start()
-
-    @pl.when(is_mid)
-    def _():
-        for n, dst in mid_sends:
-            own(n, dst).start()
-        up[pl.ds(pl.multiple_of(me * ur, 16), ur)] = up_shard[...]
-        down[pl.ds(pl.multiple_of(me * dr, 16), dr)] = down_shard[...]
+    def begin():
+        @pl.when(is_end)
+        def _():
+            for n, dst in end_sends:
+                piece(n, me, dst).start()
+
+        @pl.when(is_mid)
+        def _():
+            for n, dst in mid_sends:
+                piece(n, me, dst).start()
 
     def relay(part):
         @pl.when(is_end)
         def _():
             piece("ey_" + part, E_o, E_o).wait_recv()
             piece("ezo_" + part, E_o, A_y).start()
+            if part == "d":
+                piece("ezo_r", E_o, A_y).start()
             if part == "u":
                 piece("det1", A_y, E_o).wait_recv()
                 piece("det2", A_y, E_o).start()
@@ -341,6 +340,29 @@
             piece("ame_" + part, E_y, B_y).start()
             piece("am_" + part, B_y, A_o).wait_recv()
             piece("ayf_" + part, B_y, A_o).start()
+
+    def third():
+        @pl.when(is_mid)
+        def _():
+            piece("ame_u", F_y, A_o).wait_recv()
+            piece("aye_u", F_y, A_o).start()
+
+    def fourth():
+        @pl.when(is_mid)
+        def _():
+            piece("ezo_d", E_o, B_y).wait_recv()
+            piece("amo", E_o, B_y).start()
+            piece("ame_d", F_y, A_o).wait_recv()
+            piece("aye_d", F_y, A_o).start()
+
+    sibling = sec + 1 - 2 * core
+
+    for c in shards:
+        c.wait()
+
+    @pl.when(core == 0)
+    def _():
+        begin()
 
     for k in range(seq_len):
         tiled_in[k * CH : (k + 1) * CH] = embed_in[...]
@@ -376,7 +398,8 @@
         rows = rows + jnp.where(label == float(whole + k), rest[k : k + 1], 0.0)
     labs[0] = rows
     labs[1] = jnp.broadcast_to(rest[classes - whole : classes - whole + 1], (total, model))
-    scond[...] = wave[0] + rows + guide * guide_vec[...]
+    vector = jnp.concatenate([guide_vec[k : k + 1] for k in range(model // 128)], axis=1)
+    scond[...] = wave[0] + rows + guide * vector
 
     block = seq_len // 2
     blocks = 4
@@ -420,25 +443,41 @@
         parts[here] = dot32(hidden, stud_down[...]).astype(jnp.bfloat16)
         return carry
 
-    lax.fori_loop(0, blocks, front, 0)
+    lax.fori_loop(0, blocks // 2, front, 0)
+
+    @pl.when(core == 0)
+    def _():
+        relay("u")
+
+    lax.fori_loop(blocks // 2, blocks, front, 0)
 
     half_rows = seq_len * total // 2
 
     def half_of(ref, c):
         return ref.at[pl.ds(pl.multiple_of(c * half_rows, half_rows), half_rows)]
 
-    sibling = sec + 1 - 2 * core
     pair = copy(index["pair"], half_of(parts, 1 - core), pair_in, section=sibling)
     cross = copy(index["cross"], pair_sum, cross_in, section=lax.rem(sec + 2, sections))
     back = copy(index["back"], half_of(mixed, core), half_of(mixed, core), section=sibling)
     pair.start()
-    relay("u")
+
+    @pl.when(core == 0)
+    def _():
+        relay("d")
+        pl.semaphore_signal(
+            gate, inc=1, device_id={"section": sibling}, device_id_type=MESH
+        )
+
     pair.wait_recv()
     pair_sum[...] = (
         half_of(parts, core)[...].astype(jnp.float32) + pair_in[...].astype(jnp.float32)
     ).astype(jnp.bfloat16)
     cross.start()
-    relay("d")
+
+    @pl.when(core == 0)
+    def _():
+        third()
+
     turned = model // 4
 
     def turn(i, carry):
@@ -453,10 +492,15 @@
 
     lax.fori_loop(0, 4, turn, 0)
 
-    @pl.when(is_mid)
-    def _():
-        piece("ame_u", F_y, A_o).wait_recv()
-        piece("aye_u", F_y, A_o).start()
+    @pl.when(core == 0)
+    def _():
+        fourth()
+
+    @pl.when(core == 1)
+    def _():
+        pl.semaphore_wait(gate, 1)
+        begin()
+        relay("u")
 
     cross.wait_recv()
     mixed[pl.ds(pl.multiple_of(core * half_rows, half_rows), half_rows)] = (
@@ -464,12 +508,9 @@
     ).astype(jnp.bfloat16)
     back.start()
 
-    @pl.when(is_mid)
-    def _():
-        piece("ezo_d", E_o, B_y).wait_recv()
-        piece("amo", E_o, B_y).start()
-        piece("ame_d", F_y, A_o).wait_recv()
-        piece("aye_d", F_y, A_o).start()
+    @pl.when(core == 1)
+    def _():
+        relay("d")
 
     back.wait_recv()
     pred[...] = jnp.zeros_like(pred)
@@ -490,7 +531,17 @@
         )
         return carry
 
-    lax.fori_loop(0, blocks, middle, 0)
+    lax.fori_loop(0, blocks // 2, middle, 0)
+
+    @pl.when(core == 1)
+    def _():
+        third()
+
+    lax.fori_loop(blocks // 2, blocks, middle, 0)
+
+    @pl.when(core == 1)
+    def _():
+        fourth()
 
     trows = micro * seq_len
     chunk = 768 if up.shape[1] % 768 == 0 else up.shape[1]
@@ -525,10 +576,7 @@
 
     @pl.when(is_mid)
     def _():
-        for n, who in (
-            ("ay_u", A_o), ("ay_d", A_o), ("det3", A_o), ("ayf_u", B_o), ("ayf_d", B_o),
-            ("ezo_u", E_o), ("aye_u", F_o), ("aye_d", F_o), ("amo", F_o),
-        ):
+        for n, who in (("ay_u", A_o), ("ayf_u", B_o), ("ezo_u", E_o), ("aye_u", F_o)):
             piece(n, who, A_o).wait_recv()
         for j in range(2):
             latents[0, j] = noised[sample_rows(owned(j))]
@@ -564,6 +612,15 @@
                 hid[:, k * chunk : (k + 1) * chunk] = jax.nn.gelu(
                     dot32(normed, up[:, k * chunk : (k + 1) * chunk]), approximate=True
                 ).astype(jnp.bfloat16)
+
+            @pl.when(i == 0)
+            def _():
+                for n, who in (
+                    ("ay_d", A_o), ("det3", A_o), ("ayf_d", B_o), ("aye_d", F_o), ("amo", F_o),
+                    ("ezo_r", E_o),
+                ):
+                    piece(n, who, A_o).wait_recv()
+
             acc = dot32(hid[...], down[...])
             out = residual.reshape(seq_len, micro, model) + gate[None] * acc.reshape(
                 seq_len, micro, model
@@ -664,16 +721,17 @@
     @pl.when(is_end)
     def _():
         for n, dst in end_sends:
-            own(n, dst).wait_send()
+            piece(n, me, dst).wait_send()
         for n, who, dst in (
-            ("ezo_u", E_o, A_y), ("ezo_d", E_o, A_y), ("det2", A_y, E_o), ("det3", A_o, A_y)
+            ("ezo_u", E_o, A_y), ("ezo_d", E_o, A_y), ("ezo_r", E_o, A_y),
+            ("det2", A_y, E_o), ("det3", A_o, A_y),
         ):
             piece(n, who, dst).wait_send()
 
     @pl.when(is_mid)
     def _():
         for n, dst in mid_sends:
-            own(n, dst).wait_send()
+            piece(n, me, dst).wait_send()
         for n, who, dst in (
             ("ame_u", E_y, B_y), ("ame_d", E_y, B_y), ("amo", E_o, B_y),
             ("ayf_u", B_y, A_o), ("ayf_d", B_y, A_o), ("aye_u", F_y, A_o), ("aye_d", F_y, A_o),
@@ -728,7 +786,7 @@
             jax.ShapeDtypeStruct((share_up, stud_up.shape[1]), f32),
             jax.ShapeDtypeStruct((share_down, model), f32),
         ),
-        in_specs=[smem] * 3 + [vmem] * (len(operands) - 6) + [hbm] * 3,
+        in_specs=[smem] * 3 + [vmem] * 2 + [hbm] * 2 + [vmem] * (len(operands) - 10) + [hbm] * 3,
         out_specs=(vmem,) * 3,
         scratch_shapes=[
             V(stud_up.shape, bf16), V(stud_down.shape, bf16), V(table.shape, bf16),
@@ -746,8 +804,8 @@
             V((8, trows, model), bf16), V((8, trows, model), bf16),
             V((2, 2, micro, width), f32), V((2, micro, width), f32), V((dps, micro, width), f32),
             V((trows, hidden), bf16),
-            D((3,)), D((32,)), D((32,)), D((8,)), D((8,)), D((2,)), D((2,)),
-            D((2 * sections * dps,)), D((dps,)),
+            D((5,)), D((32,)), D((32,)), D((8,)), D((8,)), D((2,)), D((2,)),
+            D((2 * sections * dps,)), D((dps,)), pltpu.SemaphoreType.REGULAR,
         ],
         compiler_params=pltpu.CompilerParams(
             collective_id=0, has_side_effects=True, vmem_limit_bytes=63 << 20
@@ -794,6 +852,7 @@
         and micro == 8
         and seq_len % 4 == 0
         and width % 128 == 0
+        and model_width % 128 == 0
         and teacher_up.shape[1] % 16 == 0
         and teacher_down.shape[1] % 16 == 0
         and student_up.shape[1] == student_down.shape[0] == model_width
@@ -808,7 +867,7 @@
                 step_index, labels, guide_level, clean_latent, noise_draw,
                 teacher_up[0], teacher_down[0],
                 teacher_gain.reshape(3, 1, model_width), teacher_bias.reshape(3, 1, model_width),
-                student_gain, student_bias, guide_vec[None], jnp.asarray(frequency),
+                student_gain, student_bias, guide_vec.reshape(model_width // 128, 128), jnp.asarray(frequency),
                 embed_in, embed_out.T, student_up, student_down, class_table,
             ),
         )

time: 144 us -> 139 us (0.965)
  Pallas kernels: 141 us -> 138 us
    pallas_call x1, Pallas kernels: 139 us -> 136 us  [mega_call(): pl.pallas_call(functools.partial(mega_kernel, dims), out_shape=(jax.Shape...]
where the time goes in v2:
time: 139 us
  Pallas kernels  138 us (99%)
    pallas_call x1, Pallas kernels, mega_call(): pl.pallas_call(functools.partial(mega_kernel, dims), out_shape=(jax.Shape...  136 us

profile of v2, /device:TPU:0, one launch (start us, length us, event | category | flops | bytes accessed | tf_op | source)
XLA Modules:
  0.0 139.1 jit_solution(1214674681559847201)
XLA Ops:
  0.6 136.0 %shard_map.193 = (f32[8,256]{1,0:T(8,128)}, f32[144,1152]{1,0:T(8,128)}, f32[144,1152]{1,0:T(8,128)}) custom-call(s32[8]{0:T(128)} %steps_in.1, s32[8]{0:T(128)} %labels_in.1, s32[8]{0:T(128)} %levels_in.1, f32[8,256]{1,0:T(8,128)} %clean_in.1, f32[8,256]{1,0:T(8,128)} %noise_in.1, bf16[144,2304]{1,0:T(8,128)(2,1)} %bitcast.6, bf16[288,1152]{1,0:T(8,128)(2,1)} %bitcast.7, ...), custom_call_target="tpu_custom_call" | custom-call | tf_op jit(solution)/shard_map/pallas_call | solution.py:782
  136.6 2.4 %shard_map.194 = (f32[8,256]{1,0:T(8,128)}, f32[144,1152]{1,0:T(8,128)}, f32[144,1152]{1,0:T(8,128)}) custom-call(f32[8,256]{1,0:T(8,128)} %get-tuple-element.6.a, f32[144,1152]{1,0:T(8,128)} %get-tuple-element.7.b, f32[144,1152]{1,0:T(8,128)} %get-tuple-element.8.c), custom_call_target="tpu_custom_call" | custom-call | tf_op jit(solution)/shard_map/pallas_call | solution.py:814

commit v3 on v2

--- a/solution.py
+++ b/solution.py
@@ -201,14 +201,20 @@
 
 def mega_kernel(
     dims,
-    steps_in, labels_in, levels_in, clean_in, noise_in, up_shard, down_shard, t_gain, t_bias, s_gain, s_bias, guide_vec, freq,
-    embed_in, embed_out_t, stud_up_hbm, stud_down_hbm, table_hbm,
-    target_out, grad_up, grad_down,
+    steps_hbm, labels_hbm, levels_hbm, clean_in, noise_in, up_shard, down_shard,
+    *rest_refs,
+):
+    small_hbm, rest_refs = rest_refs[:8], rest_refs[8:]
+    stud_up_hbm, stud_down_hbm, table_hbm, target_out, grad_up, grad_down = rest_refs[:6]
+    steps_in, labels_in, levels_in = rest_refs[6:9]
+    small, rest_refs = rest_refs[9:17], rest_refs[17:]
+    t_gain, t_bias, s_gain, s_bias, guide_vec, freq, embed_in, embed_out_t = small
+    (
     stud_up, stud_down, table, packed, up, down, tiled_in, tiled_out,
     noised, cols, wave, labs, scond, tok, slope, n_share, h_share, parts, pair_in, pair_sum,
     cross_in, mixed, xhat, rstd, pred, states, outs, latents, velo, target_all, hid,
-    local_sem, send, recv, move_send, move_recv, z_send, z_recv, t_send, t_recv, gate,
-):
+    local_sem, send, recv, move_send, move_recv, z_send, z_recv, t_send, t_recv, near,
+    ) = rest_refs
     sections, dps, micro, seq_len = dims
     total = dps * micro
     width = clean_in.shape[1]
@@ -233,29 +239,31 @@
 
     barrier = pltpu.get_barrier_semaphore()
 
-    def greet(k, carry):
-        other = lax.rem(mine + k, devices)
-        pl.semaphore_signal(
-            barrier, inc=1, device_id={"section": other // dps, "dp": lax.rem(other, dps)},
-            device_id_type=MESH,
-        )
-        return carry
+    peer_y = z * 2 + oy
+
+    def hello(semaphore, **device):
+        pl.semaphore_signal(semaphore, inc=1, device_id=device, device_id_type=MESH)
+
+    sibling = sec + 1 - 2 * core
+    opposite = lax.rem(sec + 2, sections)
+    hello(barrier, dp=peer_y)
+    hello(barrier, section=sibling)
+    hello(barrier, section=opposite)
+
+    @pl.when(is_mid)
+    def _():
+        hello(barrier, dp=E_y)
+        hello(barrier, dp=B_y)
+
+    @pl.when(is_end)
+    def _():
+        hello(barrier, dp=A_y)
 
     def place(who):
         zz, yy = who // 2, who % 2
         return (zz % 2) * (dps // 2) + (zz // 2) * 2 + yy
 
-    lax.fori_loop(1, devices, greet, 0)
-    row = lax.broadcasted_iota(jnp.int32, (micro, 128), 0)
-    column = lax.broadcasted_iota(jnp.int32, (micro, 128), 1)
-    cells = jnp.zeros((micro, 128), jnp.float32)
-    for k, ref in enumerate((steps_in, labels_in, levels_in)):
-        for b in range(micro):
-            cells = jnp.where((row == b) & (column == k), ref[b].astype(jnp.float32), cells)
     slot = place(me)
-    packed[slot, :, 0:width] = clean_in[...]
-    packed[slot, :, width : 2 * width] = noise_in[...]
-    packed[slot, :, 2 * width :] = cells
     locals_ = [
         pltpu.make_async_copy(stud_up_hbm, stud_up, local_sem.at[0]),
         pltpu.make_async_copy(stud_down_hbm, stud_down, local_sem.at[1]),
@@ -273,9 +281,29 @@
         pltpu.make_async_copy(up_shard, urow(me), local_sem.at[3]),
         pltpu.make_async_copy(down_shard, drow(me), local_sem.at[4]),
     ]
-    for c in shards + locals_:
+    first = [
+        pltpu.make_async_copy(src, dst, local_sem.at[5 + k])
+        for k, (src, dst) in enumerate(
+            (
+                (steps_hbm, steps_in), (labels_hbm, labels_in), (levels_hbm, levels_in),
+                (clean_in, packed.at[slot, :, pl.ds(0, width)]),
+                (noise_in, packed.at[slot, :, pl.ds(width, width)]),
+            )
+        )
+    ]
+    later = [
+        pltpu.make_async_copy(src, dst, local_sem.at[10 + k])
+        for k, (src, dst) in enumerate(zip(small_hbm, small))
+    ]
+    for c in shards + later + locals_:
         c.start()
-    pl.semaphore_wait(barrier, devices - 1)
+
+    @pl.when(core == 1)
+    def _():
+        for c in first:
+            c.start()
+
+    pl.semaphore_wait(barrier, 4 + jnp.where(is_mid, 1, 0))
 
     def copy(i, src, dst, **device):
         return pltpu.make_async_remote_copy(
@@ -287,13 +315,11 @@
         copy(k - 1, packed.at[slot], packed.at[slot], dp=lax.rem(me + k, dps))
         for k in range(1, dps)
     ]
-    for c in packs:
-        c.start()
     base = dps - 1
     names = [
         "ey_u", "ey_d", "ez_u", "ez_d", "ezo_u", "ezo_d", "ezo_r", "det1", "det2", "det3",
         "ay_u", "ay_d", "am_u", "am_d", "ame_u", "ame_d", "amo",
-        "ayf_u", "ayf_d", "aye_u", "aye_d", "pair", "cross", "back",
+        "ayf_u", "ayf_d", "aye_u", "aye_d", "pair", "cross", "back", "hand",
     ]
     index = {n: base + k for k, n in enumerate(names)}
     cut = (2 * dr // 3) // 16 * 16
@@ -304,6 +330,7 @@
         ref = urow(who) if name.endswith("u") else drow(who, *span.get(name, (0, dr)))
         return copy(index[name], ref, ref, dp=dst)
 
+    hand = copy(index["hand"], packed, packed, section=sibling)
     end_sends = (("ez_u", A_y), ("ey_u", E_o), ("ez_d", A_y), ("ey_d", E_o))
     mid_sends = (
         ("am_u", B_y), ("ay_u", A_o), ("det1", E_y), ("am_d", B_y), ("ay_d", A_o)
@@ -355,8 +382,6 @@
             piece("ame_d", F_y, A_o).wait_recv()
             piece("aye_d", F_y, A_o).start()
 
-    sibling = sec + 1 - 2 * core
-
     for c in shards:
         c.wait()
 
@@ -364,13 +389,55 @@
     def _():
         begin()
 
+    @pl.when(is_mid)
+    def _():
+        hello(near.at[0], dp=B_y)
+        pl.semaphore_wait(near.at[0], 1)
+        hello(near.at[0], dp=E_y)
+
+    @pl.when(is_end)
+    def _():
+        pl.semaphore_wait(near.at[0], 1)
+
+    hello(near.at[1], dp=peer_y)
+    pl.semaphore_wait(near.at[1], 1)
+
+    @pl.when(core == 1)
+    def _():
+        for c in first:
+            c.wait()
+        row = lax.broadcasted_iota(jnp.int32, (micro, 128), 0)
+        column = lax.broadcasted_iota(jnp.int32, (micro, 128), 1)
+        cells = jnp.zeros((micro, 128), jnp.float32)
+        for k, ref in enumerate((steps_in, labels_in, levels_in)):
+            for b in range(micro):
+                cells = jnp.where((row == b) & (column == k), ref[b].astype(jnp.float32), cells)
+        packed[slot, :, 2 * width :] = cells
+        for c in packs:
+            c.start()
+
+    hello(near.at[2], section=opposite)
+    for c in later:
+        c.wait()
+    pl.semaphore_wait(near.at[2], 1)
+    hello(near.at[3], section=sibling)
+    pl.semaphore_wait(near.at[3], 1)
     for k in range(seq_len):
         tiled_in[k * CH : (k + 1) * CH] = embed_in[...]
         tiled_out[k * CH : (k + 1) * CH] = embed_out_t[...]
     lane_model = lax.broadcasted_iota(jnp.int32, (1, model), 1)
     sine_lane = jnp.where(lane_model >= model // 2, 1.0, 0.0)
-    for c in packs:
-        c.wait_recv()
+
+    @pl.when(core == 1)
+    def _():
+        for c in packs:
+            c.wait_recv()
+        hand.start()
+
+    @pl.when(core == 0)
+    def _():
+        hand.wait_recv()
+
     data = packed[...].reshape(total, packed.shape[2])
     steps = data[:, 2 * width : 2 * width + 1]
     label = data[:, 2 * width + 1 : 2 * width + 2]
@@ -443,11 +510,16 @@
         parts[here] = dot32(hidden, stud_down[...]).astype(jnp.bfloat16)
         return carry
 
+    @pl.when(core == 1)
+    def _():
+        begin()
+
     lax.fori_loop(0, blocks // 2, front, 0)
 
     @pl.when(core == 0)
     def _():
         relay("u")
+
 
     lax.fori_loop(blocks // 2, blocks, front, 0)
 
@@ -457,16 +529,17 @@
         return ref.at[pl.ds(pl.multiple_of(c * half_rows, half_rows), half_rows)]
 
     pair = copy(index["pair"], half_of(parts, 1 - core), pair_in, section=sibling)
-    cross = copy(index["cross"], pair_sum, cross_in, section=lax.rem(sec + 2, sections))
+    cross = copy(index["cross"], pair_sum, cross_in, section=opposite)
     back = copy(index["back"], half_of(mixed, core), half_of(mixed, core), section=sibling)
     pair.start()
 
     @pl.when(core == 0)
     def _():
         relay("d")
-        pl.semaphore_signal(
-            gate, inc=1, device_id={"section": sibling}, device_id_type=MESH
-        )
+
+    @pl.when(core == 1)
+    def _():
+        relay("u")
 
     pair.wait_recv()
     pair_sum[...] = (
@@ -498,9 +571,7 @@
 
     @pl.when(core == 1)
     def _():
-        pl.semaphore_wait(gate, 1)
-        begin()
-        relay("u")
+        relay("d")
 
     cross.wait_recv()
     mixed[pl.ds(pl.multiple_of(core * half_rows, half_rows), half_rows)] = (
@@ -510,7 +581,7 @@
 
     @pl.when(core == 1)
     def _():
-        relay("d")
+        third()
 
     back.wait_recv()
     pred[...] = jnp.zeros_like(pred)
@@ -533,15 +604,12 @@
 
     lax.fori_loop(0, blocks // 2, middle, 0)
 
+    lax.fori_loop(blocks // 2, blocks, middle, 0)
+
     @pl.when(core == 1)
     def _():
-        third()
-
-    lax.fori_loop(blocks // 2, blocks, middle, 0)
-
-    @pl.when(core == 1)
-    def _():
         fourth()
+
 
     trows = micro * seq_len
     chunk = 768 if up.shape[1] % 768 == 0 else up.shape[1]
@@ -715,8 +783,13 @@
 
     target_out[...] = target_all[slot]
 
-    for c in packs + [pair, cross, back]:
+    for c in (pair, cross, back):
         c.wait_send()
+
+    @pl.when(core == 1)
+    def _():
+        for c in packs + [hand]:
+            c.wait_send()
 
     @pl.when(is_end)
     def _():
@@ -776,8 +849,7 @@
     share_up, share_down = model // dps, stud_down.shape[0] // dps
     f32, bf16 = jnp.float32, jnp.bfloat16
     vmem = pl.BlockSpec(memory_space=pltpu.VMEM)
-    hbm = pl.BlockSpec(memory_space=pl.ANY)
-    smem = pl.BlockSpec(memory_space=pltpu.SMEM)
+    hbm = pl.BlockSpec(memory_space=pltpu.HBM)
     V, D = pltpu.VMEM, pltpu.SemaphoreType.DMA
     results = pl.pallas_call(
         functools.partial(mega_kernel, dims),
@@ -786,9 +858,11 @@
             jax.ShapeDtypeStruct((share_up, stud_up.shape[1]), f32),
             jax.ShapeDtypeStruct((share_down, model), f32),
         ),
-        in_specs=[smem] * 3 + [vmem] * 2 + [hbm] * 2 + [vmem] * (len(operands) - 10) + [hbm] * 3,
+        in_specs=[hbm] * len(operands),
         out_specs=(vmem,) * 3,
         scratch_shapes=[
+            *[pltpu.SMEM(a.shape, a.dtype) for a in operands[:3]],
+            *[V(a.shape, a.dtype) for a in operands[7:15]],
             V(stud_up.shape, bf16), V(stud_down.shape, bf16), V(table.shape, bf16),
             V((dps, micro, 2 * width + 128), f32),
             V((up_shard.shape[0] * dps, hidden), bf16),
@@ -804,8 +878,9 @@
             V((8, trows, model), bf16), V((8, trows, model), bf16),
             V((2, 2, micro, width), f32), V((2, micro, width), f32), V((dps, micro, width), f32),
             V((trows, hidden), bf16),
-            D((5,)), D((32,)), D((32,)), D((8,)), D((8,)), D((2,)), D((2,)),
-            D((2 * sections * dps,)), D((dps,)), pltpu.SemaphoreType.REGULAR,
+            D((18,)), D((40,)), D((40,)), D((8,)), D((8,)), D((2,)), D((2,)),
+            D((2 * sections * dps,)), D((dps,)),
+            pltpu.SemaphoreType.REGULAR((4,)),
         ],
         compiler_params=pltpu.CompilerParams(
             collective_id=0, has_side_effects=True, vmem_limit_bytes=63 << 20

time: 139 us -> 134 us (0.964)
  Pallas kernels: 138 us -> 134 us
    pallas_call x1, Pallas kernels: 136 us -> 131 us  [mega_call(): pl.pallas_call(functools.partial(mega_kernel, dims), out_shape=(jax.Shape...]
where the time goes in v3:
time: 134 us
  Pallas kernels  134 us (100%)
    pallas_call x1, Pallas kernels, mega_call(): pl.pallas_call(functools.partial(mega_kernel, dims), out_shape=(jax.Shape...  131 us

profile of v3, /device:TPU:0, one launch (start us, length us, event | category | flops | bytes accessed | tf_op | source)
XLA Modules:
  0.0 134.2 jit_solution(10883207692183225870)
XLA Ops:
  0.6 131.2 %shard_map.193 = (f32[8,256]{1,0:T(8,128)}, f32[144,1152]{1,0:T(8,128)}, f32[144,1152]{1,0:T(8,128)}) custom-call(s32[8]{0:T(128)} %steps_hbm.1, s32[8]{0:T(128)} %labels_hbm.1, s32[8]{0:T(128)} %levels_hbm.1, f32[8,256]{1,0:T(8,128)} %clean_in.1, f32[8,256]{1,0:T(8,128)} %noise_in.1, bf16[144,2304]{1,0:T(8,128)(2,1)} %bitcast.6, bf16[288,1152]{1,0:T(8,128)(2,1)} %bitcast.7, ...), custom_call_target="tpu_custom_call" | custom-call | tf_op jit(solution)/shard_map/pallas_call | solution.py:854
  131.8 2.4 %shard_map.194 = (f32[8,256]{1,0:T(8,128)}, f32[144,1152]{1,0:T(8,128)}, f32[144,1152]{1,0:T(8,128)}) custom-call(f32[8,256]{1,0:T(8,128)} %get-tuple-element.6.a, f32[144,1152]{1,0:T(8,128)} %get-tuple-element.7.b, f32[144,1152]{1,0:T(8,128)} %get-tuple-element.8.c), custom_call_target="tpu_custom_call" | custom-call | tf_op jit(solution)/shard_map/pallas_call | solution.py:889

commit v4 on v3

--- a/solution.py
+++ b/solution.py
@@ -468,8 +468,8 @@
     vector = jnp.concatenate([guide_vec[k : k + 1] for k in range(model // 128)], axis=1)
     scond[...] = wave[0] + rows + guide * vector
 
-    block = seq_len // 2
-    blocks = 4
+    block = seq_len
+    blocks = 2
     group = total // 2
     brows = block * group
     share = n_share.shape[0]
@@ -483,10 +483,10 @@
         return pl.ds(pl.multiple_of(i * brows, brows), brows)
 
     def members(i):
-        return pl.ds(pl.multiple_of((i // 2) * group, group), group)
+        return pl.ds(pl.multiple_of(i * group, group), group)
 
     def first_of(i):
-        return lax.rem(i, 2) * block
+        return 0
 
     def student_part(i, k):
         return scond[members(i)] * s_gain[k : k + 1] + s_bias[k : k + 1]
@@ -612,7 +612,7 @@
 
 
     trows = micro * seq_len
-    chunk = 768 if up.shape[1] % 768 == 0 else up.shape[1]
+    chunk = up.shape[1]
 
     def owned(j):
         return j * (dps // 2) + (z - 1) * 2 + y
@@ -779,7 +779,7 @@
         seed_hi = seed.astype(jnp.bfloat16).astype(jnp.float32)
         pred[these] = seed_hi
         noised[these] = seed - seed_hi
-        lax.fori_loop(2 * part, 2 * part + 2, finish, 0)
+        lax.fori_loop(part, part + 1, finish, 0)
 
     target_out[...] = target_all[slot]
 
@@ -831,10 +831,22 @@
                 lax.fori_loop(1, devices, told, 0)
 
 
-def flush_kernel(a, b, c, x, y, z):
-    x[...] = a[...]
-    y[...] = b[...]
-    z[...] = c[...]
+def flush_kernel(a, b, c, x, y, z, u, v, w, sems):
+    reads = [
+        pltpu.make_async_copy(src, mid, sems.at[k])
+        for k, (src, mid) in enumerate(((a, u), (b, v), (c, w)))
+    ]
+    writes = [
+        pltpu.make_async_copy(mid, dst, sems.at[3 + k])
+        for k, (mid, dst) in enumerate(((u, x), (v, y), (w, z)))
+    ]
+    for c in reads:
+        c.start()
+    for c, d in zip(reads, writes):
+        c.wait()
+        d.start()
+    for d in writes:
+        d.wait()
 
 
 def mega_call(dims, operands):
@@ -889,8 +901,9 @@
     return pl.pallas_call(
         flush_kernel,
         out_shape=tuple(jax.ShapeDtypeStruct(r.shape, r.dtype) for r in results),
-        in_specs=[vmem] * 3,
-        out_specs=(vmem,) * 3,
+        in_specs=[hbm] * 3,
+        out_specs=(hbm,) * 3,
+        scratch_shapes=[V(r.shape, r.dtype) for r in results] + [D((6,))],
     )(*results)
 
 

time: 134 us -> 134 us (level)
  no operation moved by 1% of the time
where the time goes in v4:
time: 134 us
  Pallas kernels  133 us (99%)
    pallas_call x1, Pallas kernels, mega_call(): pl.pallas_call(functools.partial(mega_kernel, dims), out_shape=(jax.Shape...  131 us

profile of v4, /device:TPU:0, one launch (start us, length us, event | category | flops | bytes accessed | tf_op | source)
XLA Modules:
  0.0 133.7 jit_solution(4911407193498836100)
XLA Ops:
  0.6 130.6 %shard_map.193 = (f32[8,256]{1,0:T(8,128)}, f32[144,1152]{1,0:T(8,128)}, f32[144,1152]{1,0:T(8,128)}) custom-call(s32[8]{0:T(128)} %steps_hbm.1, s32[8]{0:T(128)} %labels_hbm.1, s32[8]{0:T(128)} %levels_hbm.1, f32[8,256]{1,0:T(8,128)} %clean_in.1, f32[8,256]{1,0:T(8,128)} %noise_in.1, bf16[144,2304]{1,0:T(8,128)(2,1)} %bitcast.6, bf16[288,1152]{1,0:T(8,128)(2,1)} %bitcast.7, ...), custom_call_target="tpu_custom_call" | custom-call | tf_op jit(solution)/shard_map/pallas_call | solution.py:866
  131.3 2.2 %shard_map.194 = (f32[8,256]{1,0:T(8,128)}, f32[144,1152]{1,0:T(8,128)}, f32[144,1152]{1,0:T(8,128)}) custom-call(f32[8,256]{1,0:T(8,128)} %get-tuple-element.6.a, f32[144,1152]{1,0:T(8,128)} %get-tuple-element.7.b, f32[144,1152]{1,0:T(8,128)} %get-tuple-element.8.c), custom_call_target="tpu_custom_call" | custom-call | tf_op jit(solution)/shard_map/pallas_call | solution.py:901
